TPU v7x, 32 devices: a whole 2x2x4 slice. The times are simulated.
32 devices in a mesh: dp: 8 (over y, x, core), mp: 4 (over z).
Axes of the slice: x: 2, y: 2, z: 4, core: 2. Of those that a mesh axis runs over, the one named last changes fastest.
Arguments:
- tokens: bfloat16 [4096, 1024], P('dp', 'mp'), may hold values from -150 to 150
- pre_gain: bfloat16 [1024], P('mp'), may hold values from 0.25 to 1.75
- input_weight: bfloat16 [3, 1024, 1024], P(None, 'dp', 'mp'), may hold values from -0.125 to 0.125
- output_weight: bfloat16 [1024, 1024], P('mp', 'dp'), may hold values from -1 to 1
- position_bias: bfloat16 [16, 512, 512], P('mp'), may hold values from -3 to 353
- post_gain: bfloat16 [1024], P('mp'), may hold values from 0.25 to 1.75
Outputs:
- stream: bfloat16 [4096, 1024], P('dp', 'mp')
- normed: bfloat16 [4096, 1024], P('dp', 'mp')
All inputs are finite; a program needn't handle non-finite values.
Results may differ from a plain program's by a relative error of at most 0.013.
Values may be sent and summed in bfloat16 or wider, within the bound.
A program may use at most 64 MiB of HBM per device.

v0:
```python
import functools

import jax
import jax.numpy as jnp
from jax import lax
from jax.experimental import pallas as pl
from jax.experimental.pallas import tpu as pltpu
from jax.sharding import PartitionSpec as P

epsilon = 1e-06
F32, BF16 = jnp.float32, jnp.bfloat16


def kernel(
    n,
    groups,
    chunks,
    lag,
    wide,
    tok,
    pre,
    win,
    wout,
    bias,
    stream_o,
    square_o,
    x_all,
    gain_all,
    w_all,
    wo_all,
    bias_v,
    acc,
    square,
    qkv,
    part,
    out_buf,
    from_below,
    from_above,
    ss_mine,
    ss_all,
    ag_send,
    ag_recv,
    g_send,
    g_recv,
    w_send,
    w_recv,
    o_send,
    o_recv,
    rs_send,
    rs_recv,
    ss_send,
    ss_recv,
    local_sem,
    link_free,
):
    rows, feats = tok.shape
    step = rows // chunks
    heads, seq = bias.shape[0], bias.shape[1]
    inner = win.shape[2]
    head_dim = inner // heads
    model = n * feats
    wrows = win.shape[1]
    wcols = model // groups
    half = groups // 2
    me = lax.axis_index("mp")
    d = lax.axis_index("dp")
    odd = lax.rem(d, 2)
    pair = d // 2
    partner = d + 1 - 2 * odd

    def rows_at(c):
        return pl.ds(pl.multiple_of(c * step, step), step)

    def feats_at(s):
        return pl.ds(pl.multiple_of(s * feats, feats), feats)

    def tok_copy(s, c, up, own):
        src = tok.at[rows_at(c)] if own else x_all.at[s, rows_at(c)]
        return pltpu.make_async_remote_copy(
            src_ref=src,
            dst_ref=x_all.at[s, rows_at(c)],
            send_sem=ag_send.at[up, s, c],
            recv_sem=ag_recv.at[s, c],
            device_id={"mp": me + 2 * up - 1},
            device_id_type=pl.DeviceIdType.MESH,
        )

    def gain_copy(origin, target):
        return pltpu.make_async_remote_copy(
            src_ref=pre,
            dst_ref=gain_all.at[feats_at(origin)],
            send_sem=g_send.at[target],
            recv_sem=g_recv.at[origin],
            device_id={"mp": target},
            device_id_type=pl.DeviceIdType.MESH,
        )

    def w_slot(o):
        return w_all.at[:, pl.ds(pl.multiple_of(o * wrows, wrows), wrows), :]

    def o_slot(o):
        block = pl.ds(pl.multiple_of(o * wcols, wcols), wcols)
        return wo_all.at[:, block] if wide else wo_all.at[block, :]

    def weight_copy(which, o, target, forward):
        slot, ref, send, recv = (
            (w_slot, win, w_send, w_recv) if which == 0 else (o_slot, wout, o_send, o_recv)
        )
        return pltpu.make_async_remote_copy(
            src_ref=slot(o) if forward else ref,
            dst_ref=slot(o),
            send_sem=send.at[1, o] if forward else send.at[0, target],
            recv_sem=recv.at[o],
            device_id={"dp": target},
            device_id_type=pl.DeviceIdType.MESH,
        )

    def rs_copy(s, c, up):
        return pltpu.make_async_remote_copy(
            src_ref=out_buf.at[s, rows_at(c)],
            dst_ref=(from_below if up else from_above).at[s, rows_at(c)],
            send_sem=rs_send.at[s, c],
            recv_sem=rs_recv.at[up, s, c],
            device_id={"mp": me + 2 * up - 1},
            device_id_type=pl.DeviceIdType.MESH,
        )

    def ss_copy(origin, c, target):
        return pltpu.make_async_remote_copy(
            src_ref=ss_mine.at[c],
            dst_ref=ss_all.at[origin, c],
            send_sem=ss_send.at[target, c],
            recv_sem=ss_recv.at[origin, c],
            device_id={"mp": target},
            device_id_type=pl.DeviceIdType.MESH,
        )

    def loop(count, body, start=0):
        def wrapped(i, carry):
            body(i)
            return carry

        lax.fori_loop(start, count, wrapped, 0)

    def local_copies():
        return (
            pltpu.make_async_copy(win, w_slot(d), local_sem.at[0]),
            pltpu.make_async_copy(wout, o_slot(d), local_sem.at[1]),
            pltpu.make_async_copy(tok, x_all.at[me], local_sem.at[2]),
            pltpu.make_async_copy(pre, gain_all.at[feats_at(me)], local_sem.at[3]),
            pltpu.make_async_copy(bias, bias_v, local_sem.at[4]),
        )

    for copy in local_copies():
        copy.start()

    barrier = pltpu.get_barrier_semaphore()

    def greet_mp(k):
        pl.semaphore_signal(
            barrier,
            inc=1,
            device_id={"mp": lax.rem(me + k, n)},
            device_id_type=pl.DeviceIdType.MESH,
        )

    def greet_dp(k):
        pl.semaphore_signal(
            barrier,
            inc=1,
            device_id={"dp": lax.rem(d + k, groups)},
            device_id_type=pl.DeviceIdType.MESH,
        )

    loop(n, greet_mp, 1)
    loop(groups, greet_dp, 1)
    pl.semaphore_wait(barrier, n - 1 + groups - 1)

    def peer_mp(k):
        return lax.rem(me + k, n)

    def same_core(k):
        return 2 * lax.rem(pair + k, half) + odd

    def from_core(k):
        return 2 * lax.rem(pair + half - k, half) + odd

    loop(n, lambda k: gain_copy(me, peer_mp(k)).start(), 1)
    def send_own(up):
        @pl.when((me < n - 1) if up else (me > 0))
        def _():
            @pl.when(odd == 1)
            def _():
                pl.semaphore_wait(link_free.at[up], 1)

            loop(chunks, lambda c: tok_copy(me, c, up, True).start())

    def release(up):
        s = 0 if up else n - 1

        @pl.when(((me < n - 1) if up else (me > 0)) & (odd == 0))
        def _():
            loop(chunks, lambda c: tok_copy(s, c, up, False).wait_send())
            pl.semaphore_signal(
                link_free.at[up],
                inc=1,
                device_id={"dp": partner},
                device_id_type=pl.DeviceIdType.MESH,
            )

    def send_both():
        @pl.when(2 * me < n)
        def _():
            send_own(1)
            send_own(0)

        @pl.when(2 * me >= n)
        def _():
            send_own(0)
            send_own(1)

    pl.when(odd == 0)(send_both)
    weight_copy(0, d, partner, False).start()
    loop(half, lambda k: weight_copy(0, d, same_core(k), False).start(), 1)
    weight_copy(1, d, partner, False).start()
    loop(half, lambda k: weight_copy(1, d, same_core(k), False).start(), 1)

    pl.when((odd == 0) & (me == 0))(lambda: release(1))
    pl.when((odd == 0) & (me == n - 1))(lambda: release(0))

    acc[...] = jnp.zeros_like(acc)
    square[...] = jnp.zeros_like(square)

    def take_shards(j):
        below, above = me - j, me + j

        def one(c):
            @pl.when(below >= 0)
            def _():
                tok_copy(below, c, 1, False).wait_recv()

                @pl.when(me < n - 1)
                def _():
                    tok_copy(below, c, 1, False).start()

            @pl.when(above < n)
            def _():
                tok_copy(above, c, 0, False).wait_recv()

                @pl.when(me > 0)
                def _():
                    tok_copy(above, c, 0, False).start()

        loop(chunks, one)
        pl.when((j == me))(lambda: release(1))
        pl.when((j == n - 1 - me))(lambda: release(0))

    def project(j):
        def side(up):
            s = me + (2 * up - 1) * j

            @pl.when((s >= 0) & (s < n) & ((j > 0) | (up == 0)))
            def _():
                block = feats_at(s)
                gain = gain_all[feats_at(s)].astype(F32).reshape(1, feats)

                x = x_all[s].astype(F32)
                square[...] += x * x
                xg = (x * gain).astype(BF16)
                for m in range(3):
                    acc[m] += jnp.dot(xg, w_all[m, block, :], preferred_element_type=F32)

        loop(2, side)

    def forward_weights(which):
        def forward(k):
            o = from_core(k)
            weight_copy(which, o, partner, False).wait_recv()
            weight_copy(which, o, partner, True).start()

        loop(half, forward, 1)

    def other_weights(which):
        loop(half, lambda k: weight_copy(which, 2 * k + 1 - odd, partner, False).wait_recv())

    @pl.when(odd == 1)
    def _():
        forward_weights(0)
        send_both()
        take_shards(1)
        forward_weights(1)

    @pl.when(odd == 0)
    def _():
        loop(n, take_shards, 1)
        forward_weights(0)

    for copy in local_copies():
        copy.wait()
    loop(n, lambda k: gain_copy(peer_mp(k), peer_mp(k)).wait_recv(), 1)
    other_weights(0)
    loop(2, project)

    def later(j):
        pl.when(odd == 1)(lambda: take_shards(j))
        project(j)

    loop(n, later, 2)
    pl.when(odd == 0)(lambda: forward_weights(1))
    other_weights(1)

    def finish(c):
        total = jnp.sum(square[rows_at(c), :], axis=1, keepdims=True)
        inverse = lax.rsqrt(total / model + epsilon)
        for m in range(3):
            qkv[m, rows_at(c), :] = (acc[m, rows_at(c), :] * inverse).astype(BF16)

    loop(chunks, finish)

    lane_head = lax.broadcasted_iota(jnp.int32, (1, inner), 1) // head_dim
    contract = (((1,), (1,)), ((), ()))

    def send_out(s, c, up, value):
        out_buf[s, rows_at(c), :] = value.astype(BF16)
        rs_copy(s, c, up).start()

    def attend(c):
        first = (c * step) // seq * seq
        keys_at = pl.ds(pl.multiple_of(first, seq), seq)
        bias_at = pl.ds(pl.multiple_of(c * step - first, step), step)
        q = qkv[0, rows_at(c), :]
        k = qkv[1, keys_at, :]
        v = qkv[2, keys_at, :]
        context = jnp.zeros((step, inner), F32)
        for h in range(heads):
            qh = jnp.where(lane_head == h, q, jnp.zeros_like(q))
            scores = lax.dot_general(qh, k, contract, preferred_element_type=F32)
            scores = scores + bias_v[h, bias_at, :].astype(F32)
            weights = jnp.exp(scores - jnp.max(scores, axis=1, keepdims=True))
            scale = 1.0 / jnp.sum(weights, axis=1, keepdims=True)
            mixed = jnp.dot(weights.astype(BF16), v, preferred_element_type=F32)
            context = jnp.where(lane_head == h, mixed * scale, context)
        context = context.astype(BF16)

        def share(s):
            block = feats_at(s)
            if wide:
                value = jnp.dot(context, wo_all[:, block], preferred_element_type=F32)
            else:
                value = lax.dot_general(
                    context, wo_all[block, :], contract, preferred_element_type=F32
                )
            part[s, rows_at(c), :] = value

        for s in range(n):
            share(s)

        @pl.when(me == 0)
        def _():
            loop(n - 1, lambda k: send_out(n - 1 - k, c, 1, part[n - 1 - k, rows_at(c), :]))

        @pl.when(me == n - 1)
        def _():
            loop(n - 1, lambda k: send_out(k, c, 0, part[k, rows_at(c), :]))

    loop(rows // step, attend)

    def finalize(c):
        own = x_all[me, rows_at(c), :].astype(F32) + part[me, rows_at(c), :]
        stream = own.astype(BF16)
        stream_o[rows_at(c), :] = stream
        wide_stream = stream.astype(F32)
        total = jnp.sum(wide_stream * wide_stream, axis=1, keepdims=True)
        turned = jnp.transpose(jnp.broadcast_to(total, (step, 128)))
        ss_mine[c] = turned[0:8, :]
        ss_all[me, c] = turned[0:8, :]
        loop(n, lambda k: ss_copy(me, c, peer_mp(k)).start(), 1)

    messages = chunks * (n - 1)

    def chain(t, up, lead):
        m = t - lead
        landed = from_below if up else from_above

        @pl.when((m >= 0) & (m < messages))
        def _():
            c, k = m // (n - 1), lax.rem(m, n - 1)
            s = n - 1 - k if up else k
            further = s > me if up else s < me

            @pl.when(further | (s == me))
            def _():
                rs_copy(s, c, up).wait_recv()
                value = part[s, rows_at(c), :] + landed[s, rows_at(c), :].astype(F32)

                @pl.when(s == me)
                def _():
                    part[s, rows_at(c), :] = value

                @pl.when(further)
                def _():
                    send_out(s, c, up, value)

    up_lead, down_lead = (me - 1) * lag, (n - 2 - me) * lag
    up_last, down_last = n - 1 - me + up_lead, me + down_lead
    last = jnp.where(
        me == 0, down_last, jnp.where(me == n - 1, up_last, jnp.maximum(up_last, down_last))
    )

    def tick(t):
        @pl.when(me > 0)
        def _():
            chain(t, 1, up_lead)

        @pl.when(me < n - 1)
        def _():
            chain(t, 0, down_lead)

        @pl.when((t >= last) & (lax.rem(t - last + n - 1, n - 1) == 0))
        def _():
            c = (t - last + n - 1) // (n - 1) - 1

            @pl.when(c < chunks)
            def _():
                finalize(c)

    loop(messages + (n - 2) * lag, tick)

    def normalize(c):
        loop(n, lambda k: ss_copy(peer_mp(k), c, peer_mp(k)).wait_recv(), 1)
        total = jnp.zeros((8, step), F32)
        for s in range(n):
            total = total + ss_all[s, c]
        square_o[c] = total

    loop(chunks, normalize)

    loop(n, lambda k: gain_copy(me, peer_mp(k)).wait_send(), 1)

    def drain_tokens(s):
        def one(c):
            @pl.when((s <= me) & (me < n - 1) & ((s > 0) | (odd == 1)))
            def _():
                tok_copy(s, c, 1, False).wait_send()

            @pl.when((s >= me) & (me > 0) & ((s < n - 1) | (odd == 1)))
            def _():
                tok_copy(s, c, 0, False).wait_send()

            @pl.when(s != me)
            def _():
                rs_copy(s, c, 1).wait_send()
                ss_copy(me, c, s).wait_send()

        loop(chunks, one)

    loop(n, drain_tokens)
    for which in range(2):
        weight_copy(which, d, partner, False).wait_send()

        def drain(k):
            weight_copy(which, d, same_core(k), False).wait_send()
            weight_copy(which, from_core(k), partner, True).wait_send()

        loop(half, drain, 1)


def post_norm(model, stream_i, square_i, gain_i, stream_o, normed_o):
    chunks, _, step = square_i.shape
    gain = gain_i[...].astype(F32).reshape(1, stream_i.shape[1])
    for c in range(chunks):
        post = jnp.transpose(lax.rsqrt(square_i[c] / model + epsilon))[:, 0:1]
        stream = stream_i[c * step : (c + 1) * step, :]
        stream_o[c * step : (c + 1) * step, :] = stream
        normed_o[c * step : (c + 1) * step, :] = (stream.astype(F32) * post * gain).astype(BF16)


def on_device(n, groups, tokens, pre_gain, input_weight, output_weight, position_bias, post_gain):
    rows, feats = tokens.shape
    chunks, lag = rows // 256, 2
    step = rows // chunks
    inner = input_weight.shape[2]
    model = n * feats
    wide = output_weight.shape[1] % 128 == 0
    if not wide:
        output_weight = output_weight.T
    dma, any_space = pltpu.SemaphoreType.DMA, pl.BlockSpec(memory_space=pl.ANY)
    shape = jax.ShapeDtypeStruct((rows, feats), BF16)
    stream, squares = pl.pallas_call(
        functools.partial(kernel, n, groups, chunks, lag, wide),
        out_shape=(shape, jax.ShapeDtypeStruct((chunks, 8, step), F32)),
        in_specs=[any_space] * 5,
        out_specs=[pl.BlockSpec(memory_space=pltpu.VMEM)] * 2,
        scratch_shapes=[
            pltpu.VMEM((n, rows, feats), BF16),
            pltpu.VMEM((n * feats,), BF16),
            pltpu.VMEM((3, model, inner), BF16),
            pltpu.VMEM((inner, model) if wide else (model, inner), BF16),
            pltpu.VMEM(position_bias.shape, BF16),
            pltpu.VMEM((3, rows, inner), F32),
            pltpu.VMEM((rows, feats), F32),
            pltpu.VMEM((3, rows, inner), BF16),
            pltpu.VMEM((n, rows, feats), F32),
            pltpu.VMEM((n, rows, feats), BF16),
            pltpu.VMEM((n, rows, feats), BF16),
            pltpu.VMEM((n, rows, feats), BF16),
            pltpu.VMEM((chunks, 8, step), F32),
            pltpu.VMEM((n, chunks, 8, step), F32),
            dma((2, n, chunks)),
            dma((n, chunks)),
            dma((n,)),
            dma((n,)),
            dma((2, groups)),
            dma((groups,)),
            dma((2, groups)),
            dma((groups,)),
            dma((n, chunks)),
            dma((2, n, chunks)),
            dma((n, chunks)),
            dma((n, chunks)),
            dma((5,)),
            pltpu.SemaphoreType.REGULAR((2,)),
        ],
        compiler_params=pltpu.CompilerParams(
            collective_id=0, has_side_effects=True, vmem_limit_bytes=56 * 1024 * 1024
        ),
    )(tokens, pre_gain, input_weight, output_weight, position_bias)
    vmem = pl.BlockSpec(memory_space=pltpu.VMEM)
    return pl.pallas_call(
        functools.partial(post_norm, model),
        out_shape=(shape, shape),
        in_specs=[vmem] * 3,
        out_specs=[vmem] * 2,
        compiler_params=pltpu.CompilerParams(vmem_limit_bytes=8 * 1024 * 1024),
    )(stream, squares, post_gain)


def solution(mesh):
    return jax.shard_map(
        functools.partial(on_device, mesh.shape["mp"], mesh.shape["dp"]),
        mesh=mesh,
        in_specs=(
            P("dp", "mp"),
            P("mp"),
            P(None, "dp", "mp"),
            P("mp", "dp"),
            P("mp", None, None),
            P("mp"),
        ),
        out_specs=(P("dp", "mp"), P("dp", "mp")),
        check_vma=False,
    )
```

profile of v0, /device:TPU:1, one launch (start us, length us, event | category | flops | bytes accessed | tf_op | source)
XLA Modules:
  0.0 56.8 jit_solution(948782587454180523)
XLA Ops:
  0.6 0.0 copy-start.2
  0.6 53.5 %shard_map.77 = (bf16[512,256]{1,0:T(8,128)(2,1)}, f32[2,8,256]{2,1,0:T(8,128)}) custom-call(bf16[512,256]{1,0:T(8,128)(2,1)} %tok.1, bf16[256]{0:T(256)(128)(2,1)} %pre.1, bf16[3,128,256]{2,1,0:T(8,128)(2,1)} %win.1, bf16[256,128]{1,0:T(8,128)(2,1)} %wout.1, bf16[4,512,512]{2,1,0:T(8,128)(2,1)} %bias.1), custom_call_target="tpu_custom_call" | custom-call | tf_op jit(solution)/shard_map/pallas_call | solution.py:489
  54.2 0.0 copy-done.2
  54.2 0.0 copy-start
  54.2 0.9 %copy-done = bf16[512,256]{1,0:T(8,128)(2,1)S(1)} copy-done((bf16[512,256]{1,0:T(8,128)(2,1)S(1)}, bf16[512,256]{1,0:T(8,128)(2,1)}, u32[]{:S(2)}) %copy-start) | copy-done | bytes 262168
  55.1 0.0 copy-start.1
  55.1 0.7 %copy-done.1 = f32[2,8,256]{2,1,0:T(8,128)S(1)} copy-done((f32[2,8,256]{2,1,0:T(8,128)S(1)}, f32[2,8,256]{2,1,0:T(8,128)}, u32[]{:S(2)}) %copy-start.1) | copy-done | bytes 16408
  55.9 1.0 %shard_map.78 = (bf16[512,256]{1,0:T(8,128)(2,1)}, bf16[512,256]{1,0:T(8,128)(2,1)}) custom-call(bf16[512,256]{1,0:T(8,128)(2,1)S(1)} %copy-done, f32[2,8,256]{2,1,0:T(8,128)S(1)} %copy-done.1, bf16[256]{0:T(256)(128)(2,1)S(1)} %copy-done.2), custom_call_target="tpu_custom_call" | custom-call | tf_op jit(solution)/shard_map/pallas_call | solution.py:529
Async XLA Ops:
  0.6 53.5 %copy-start.2 = (bf16[256]{0:T(256)(128)(2,1)S(1)}, bf16[256]{0:T(256)(128)(2,1)}, u32[]{:S(2)}) copy-start(bf16[256]{0:T(256)(128)(2,1)} %gain_i.1) | copy-start | bytes 1540
  54.2 1.0 %copy-start = (bf16[512,256]{1,0:T(8,128)(2,1)S(1)}, bf16[512,256]{1,0:T(8,128)(2,1)}, u32[]{:S(2)}) copy-start(bf16[512,256]{1,0:T(8,128)(2,1)} %get-tuple-element.4.stream_i) | copy-start | bytes 786436
  55.1 0.7 %copy-start.1 = (f32[2,8,256]{2,1,0:T(8,128)S(1)}, f32[2,8,256]{2,1,0:T(8,128)}, u32[]{:S(2)}) copy-start(f32[2,8,256]{2,1,0:T(8,128)} %get-tuple-element.5.square_i) | copy-start | bytes 49156
where the time goes:
time: 57.1 us; the launch traced here: 56.8 us
  Pallas kernels  54.5 us (95%)
  local copies, waits for them, and re-layouts  1.66 us (3%)
  between operations  0.66 us (1%)
    pallas_call x1, Pallas kernels, on_device(): pl.pallas_call(functools.partial(kernel, n, groups, chunks, lag, wide), o...  53.5 us
    unnamed x6, local copies, waits for them, and re-layouts  1.66 us

commit v1 on v0

--- a/solution.py
+++ b/solution.py
@@ -465,14 +465,19 @@
         loop(half, drain, 1)
 
 
-def post_norm(model, stream_i, square_i, gain_i, stream_o, normed_o):
+def post_norm(model, stream_i, square_i, gain_i, stream_o, normed_o, normed_v, sems):
     chunks, _, step = square_i.shape
+    copies = [pltpu.make_async_copy(stream_i, stream_o, sems.at[0])]
+    copies[0].start()
     gain = gain_i[...].astype(F32).reshape(1, stream_i.shape[1])
     for c in range(chunks):
+        at = pl.ds(c * step, step)
         post = jnp.transpose(lax.rsqrt(square_i[c] / model + epsilon))[:, 0:1]
-        stream = stream_i[c * step : (c + 1) * step, :]
-        stream_o[c * step : (c + 1) * step, :] = stream
-        normed_o[c * step : (c + 1) * step, :] = (stream.astype(F32) * post * gain).astype(BF16)
+        normed_v[at, :] = (stream_i[at, :].astype(F32) * post * gain).astype(BF16)
+        copies.append(pltpu.make_async_copy(normed_v.at[at], normed_o.at[at], sems.at[1 + c]))
+        copies[-1].start()
+    for copy in copies:
+        copy.wait()
 
 
 def on_device(n, groups, tokens, pre_gain, input_weight, output_weight, position_bias, post_gain):
@@ -488,7 +493,7 @@
     shape = jax.ShapeDtypeStruct((rows, feats), BF16)
     stream, squares = pl.pallas_call(
         functools.partial(kernel, n, groups, chunks, lag, wide),
-        out_shape=(shape, jax.ShapeDtypeStruct((chunks, 8, step), F32)),
+        out_shape=(pltpu.VMEM((rows, feats), BF16), pltpu.VMEM((chunks, 8, step), F32)),
         in_specs=[any_space] * 5,
         out_specs=[pl.BlockSpec(memory_space=pltpu.VMEM)] * 2,
         scratch_shapes=[
@@ -530,7 +535,8 @@
         functools.partial(post_norm, model),
         out_shape=(shape, shape),
         in_specs=[vmem] * 3,
-        out_specs=[vmem] * 2,
+        out_specs=[any_space] * 2,
+        scratch_shapes=[pltpu.VMEM((rows, feats), BF16), dma((1 + chunks,))],
         compiler_params=pltpu.CompilerParams(vmem_limit_bytes=8 * 1024 * 1024),
     )(stream, squares, post_gain)
 

time: 57.1 us -> 54.6 us (0.956)
  local copies, waits for them, and re-layouts: 1.66 us -> 0.01 us
  Pallas kernels: 54.5 us -> 53.8 us
    unnamed x6 -> x2, local copies, waits for them, and re-layouts: 1.66 us -> 0.01 us
    pallas_call x1, Pallas kernels: 53.5 us -> 52.8 us  [on_device(): pl.pallas_call(functools.partial(kernel, n, groups, chunks, lag, wide), o...]
where the time goes in v1:
time: 54.6 us; the launch traced here: 54.5 us
  Pallas kernels  53.8 us (99%)
  between operations  0.66 us (1%)
    pallas_call x1, Pallas kernels, on_device(): pl.pallas_call(functools.partial(kernel, n, groups, chunks, lag, wide), o...  52.8 us

profile of v1, /device:TPU:1, one launch (start us, length us, event | category | flops | bytes accessed | tf_op | source)
XLA Modules:
  0.0 54.5 jit_solution(12812967462748371755)
XLA Ops:
  0.6 0.0 copy-start
  0.6 52.8 %shard_map.77 = (bf16[512,256]{1,0:T(8,128)(2,1)S(1)}, f32[2,8,256]{2,1,0:T(8,128)S(1)}) custom-call(bf16[512,256]{1,0:T(8,128)(2,1)} %tok.1, bf16[256]{0:T(256)(128)(2,1)} %pre.1, bf16[3,128,256]{2,1,0:T(8,128)(2,1)} %win.1, bf16[256,128]{1,0:T(8,128)(2,1)} %wout.1, bf16[4,512,512]{2,1,0:T(8,128)(2,1)} %bias.1), custom_call_target="tpu_custom_call" | custom-call | tf_op jit(solution)/shard_map/pallas_call | solution.py:494
  53.5 0.0 copy-done
  53.5 1.0 %shard_map.78 = (bf16[512,256]{1,0:T(8,128)(2,1)}, bf16[512,256]{1,0:T(8,128)(2,1)}) custom-call(bf16[512,256]{1,0:T(8,128)(2,1)S(1)} %get-tuple-element.4.stream_i, f32[2,8,256]{2,1,0:T(8,128)S(1)} %get-tuple-element.5.square_i, bf16[256]{0:T(256)(128)(2,1)S(1)} %copy-done), custom_call_target="tpu_custom_call" | custom-call | tf_op jit(solution)/shard_map/pallas_call | solution.py:534
Async XLA Ops:
  0.6 52.8 %copy-start = (bf16[256]{0:T(256)(128)(2,1)S(1)}, bf16[256]{0:T(256)(128)(2,1)}, u32[]{:S(2)}) copy-start(bf16[256]{0:T(256)(128)(2,1)} %gain_i.1) | copy-start | bytes 1540

commit v2 on v1

v2 whole, which is shorter than its diff:
```python
import functools

import jax
import jax.numpy as jnp
from jax import lax
from jax.experimental import pallas as pl
from jax.experimental.pallas import tpu as pltpu
from jax.sharding import PartitionSpec as P

epsilon = 1e-06
F32, BF16 = jnp.float32, jnp.bfloat16
MESH = pl.DeviceIdType.MESH


def kernel(
    n,
    groups,
    chunks,
    wide,
    tok,
    pre,
    win,
    wout,
    bias,
    post,
    stream_o,
    normed_o,
    x_all,
    gain_all,
    post_v,
    w_all,
    wo_all,
    wo_end,
    bias_v,
    acc,
    square,
    qkv,
    part,
    out_buf,
    landed,
    ctx_buf,
    ctx_in,
    ss_mine,
    ss_all,
    ag_send,
    ag_recv,
    g_send,
    g_recv,
    w_send,
    w_recv,
    ctx_send,
    ctx_recv,
    rs_send,
    rs_recv,
    ss_send,
    ss_recv,
    local_sem,
    link_free,
):
    rows, feats = tok.shape
    step = rows // chunks
    heads, seq = bias.shape[0], bias.shape[1]
    inner = win.shape[2]
    head_dim = inner // heads
    model = n * feats
    wrows = win.shape[1]
    wcols = model // groups
    half = groups // 2
    me = lax.axis_index("mp")
    d = lax.axis_index("dp")
    odd = lax.rem(d, 2)
    pair = d // 2
    partner = d + 1 - 2 * odd
    is_end = (me == 0) | (me == n - 1)
    is_edge = (me == 1) | (me == n - 2)
    all_rows = pl.ds(0, rows)

    def rows_at(c):
        return pl.ds(pl.multiple_of(c * step, step), step)

    def feats_at(s):
        return pl.ds(pl.multiple_of(s * feats, feats), feats)

    def loop(count, body, start=0):
        def wrapped(i, carry):
            body(i)
            return carry

        lax.fori_loop(start, count, wrapped, 0)

    def remote(src, dst, send, recv, target):
        return pltpu.make_async_remote_copy(
            src_ref=src,
            dst_ref=dst,
            send_sem=send,
            recv_sem=recv,
            device_id=target,
            device_id_type=MESH,
        )

    def tok_copy(s, c, up):
        ref = x_all.at[s, rows_at(c)]
        return remote(ref, ref, ag_send.at[up, s, c], ag_recv.at[s, c], {"mp": me + 2 * up - 1})

    def gain_copy(origin, target):
        ref = gain_all.at[feats_at(origin)]
        return remote(ref, ref, g_send.at[target], g_recv.at[origin], {"mp": target})

    def w_slot(o):
        return w_all.at[:, pl.ds(pl.multiple_of(o * wrows, wrows), wrows), :]

    def o_slot(ref, o):
        block = pl.ds(pl.multiple_of(o * wcols, wcols), wcols)
        return ref.at[:, block] if wide else ref.at[block, :]

    def slot(which, o):
        return w_slot(o) if which == 0 else o_slot(wo_all if which == 1 else wo_end, o)

    def weight_copy(which, o, target, forward):
        ref = slot(which, o)
        send = w_send.at[which, 1, o] if forward else w_send.at[which, 0, target]
        return remote(ref, ref, send, w_recv.at[which, o], {"dp": target})

    def cross_copy():
        inwards = jnp.where(me == 0, 1, n - 2)
        return remote(
            o_slot(wo_all, d), o_slot(wo_end, d), w_send.at[2, 0, d], w_recv.at[2, d], {"mp": inwards}
        )

    def ctx_copy(c):
        inwards = jnp.where(me == 0, 1, n - 2)
        return remote(
            ctx_buf.at[rows_at(c)], ctx_in.at[rows_at(c)], ctx_send.at[c], ctx_recv.at[c], {"mp": inwards}
        )

    def rs_copy(s, c, up):
        return remote(
            out_buf.at[s, rows_at(c)],
            landed.at[up, s, rows_at(c)],
            rs_send.at[s, c],
            rs_recv.at[up, s, c],
            {"mp": me + 2 * up - 1},
        )

    def ss_copy(origin, c, target):
        return remote(
            ss_mine.at[c], ss_all.at[origin, c], ss_send.at[target, c], ss_recv.at[origin, c], {"mp": target}
        )

    local = (
        pltpu.make_async_copy(tok, x_all.at[me], local_sem.at[0]),
        pltpu.make_async_copy(pre, gain_all.at[feats_at(me)], local_sem.at[1]),
        pltpu.make_async_copy(win, w_slot(d), local_sem.at[2]),
        pltpu.make_async_copy(wout, o_slot(wo_all, d), local_sem.at[3]),
        pltpu.make_async_copy(post, post_v, local_sem.at[4]),
        pltpu.make_async_copy(bias, bias_v, local_sem.at[5]),
    )
    for copy in local:
        copy.start()

    def peer_mp(k):
        return lax.rem(me + k, n)

    def same_core(k):
        return 2 * lax.rem(pair + k, half) + odd

    def from_core(k):
        return 2 * lax.rem(pair + half - k, half) + odd

    barrier = pltpu.get_barrier_semaphore()

    def greet(target):
        pl.semaphore_signal(barrier, inc=1, device_id=target, device_id_type=MESH)

    loop(n, lambda k: greet({"mp": peer_mp(k)}), 1)
    loop(half, lambda k: greet({"dp": same_core(k)}), 1)
    greet({"dp": partner})
    acc[...] = jnp.zeros_like(acc)
    square[...] = jnp.zeros_like(square)
    for copy in local[:5]:
        copy.wait()
    pl.semaphore_wait(barrier, n - 1 + half - 1 + 1)

    def can_send(up):
        return (me < n - 1) if up else (me > 0)

    def send_own(up):
        @pl.when(can_send(up))
        def _():
            @pl.when(odd == 1)
            def _():
                pl.semaphore_wait(link_free.at[up], 1)

            loop(chunks, lambda c: tok_copy(me, c, up).start())

    def release(up):
        @pl.when(can_send(up))
        def _():
            pl.semaphore_signal(
                link_free.at[up], inc=1, device_id={"dp": partner}, device_id_type=MESH
            )

    early = max(chunks - 2, 0)

    def send_weights(which):
        weight_copy(which, d, partner, False).start()
        loop(half, lambda k: weight_copy(which, d, same_core(k), False).start(), 1)

    def forward_weights(which):
        def forward(k):
            o = from_core(k)
            weight_copy(which, o, partner, False).wait_recv()
            weight_copy(which, o, partner, True).start()

        loop(half, forward, 1)

    def other_weights(which):
        loop(half, lambda k: weight_copy(which, 2 * k + 1 - odd, partner, False).wait_recv())

    def pass_end_weights():
        @pl.when(is_edge)
        def _():
            weight_copy(2, d, partner, False).wait_recv()
            send_weights(2)

    def take(up, j, use=None):
        s = me - j if up else me + j

        @pl.when((s >= 0) & (s < n))
        def _():
            def one(c):
                tok_copy(s, c, up).wait_recv()

                @pl.when(can_send(up))
                def _():
                    tok_copy(s, c, up).start()

                if use is not None:
                    use(s, c)

            loop(chunks, one)

    def accumulate(s, at):
        gain = gain_all[feats_at(s)].astype(F32).reshape(1, feats)
        x = x_all[s, at, :].astype(F32)
        square[at, :] += x * x
        xg = (x * gain).astype(BF16)
        for m in range(3):
            acc[m, at, :] += jnp.dot(xg, w_all[m, feats_at(s), :], preferred_element_type=F32)

    def gather_even():
        send_own(1)
        send_own(0)
        send_weights(0)
        pl.when(is_end)(lambda: cross_copy().start())
        pl.when(jnp.logical_not(is_end))(lambda: send_weights(1))

        @pl.when(me == 0)
        def _():
            loop(early, lambda c: tok_copy(me, c, 1).wait_send())
            release(1)

        @pl.when(me == n - 1)
        def _():
            loop(early, lambda c: tok_copy(me, c, 0).wait_send())
            release(0)

        def hop(j):
            def one(c):
                for up in (1, 0):
                    s = me - j if up else me + j

                    @pl.when((s >= 0) & (s < n))
                    def _():
                        tok_copy(s, c, up).wait_recv()
                        pl.when(can_send(up))(lambda: tok_copy(s, c, up).start())

            loop(chunks, one)
            pl.when(j == me)(lambda: release(1))
            pl.when(j == n - 1 - me)(lambda: release(0))

        loop(n, hop, 1)
        pass_end_weights()
        forward_weights(0)
        loop(n, lambda k: gain_copy(peer_mp(k), peer_mp(k)).wait_recv(), 1)
        other_weights(0)
        loop(n, lambda s: accumulate(s, all_rows))

    def gather_odd():
        send_weights(0)
        pl.when(is_end)(lambda: cross_copy().start())
        pl.when(jnp.logical_not(is_end))(lambda: send_weights(1))

        def toward(near):
            far = 1 - near
            send_own(near)
            loop(n, lambda j: take(near, j), 1)
            pass_end_weights()
            send_own(far)
            forward_weights(0)
            loop(n, lambda k: gain_copy(peer_mp(k), peer_mp(k)).wait_recv(), 1)
            take(far, 1)
            other_weights(0)

            def known(s):
                pl.when((s <= me + 1) if near else (s >= me - 1))(lambda: accumulate(s, all_rows))

            loop(n, known)

            def later(j):
                take(far, j)
                s = me + j if near else me - j
                pl.when((s >= 0) & (s < n))(lambda: accumulate(s, all_rows))

            loop(n, later, 2)

        pl.when(2 * me < n)(lambda: toward(1))
        pl.when(2 * me >= n)(lambda: toward(0))

    loop(n, lambda k: gain_copy(me, peer_mp(k)).start(), 1)
    pl.when(odd == 0)(gather_even)
    pl.when(odd == 1)(gather_odd)

    def finish(c):
        total = jnp.sum(square[rows_at(c), :], axis=1, keepdims=True)
        inverse = lax.rsqrt(total / model + epsilon)
        for m in range(3):
            qkv[m, rows_at(c), :] = (acc[m, rows_at(c), :] * inverse).astype(BF16)

    loop(chunks, finish)
    local[5].wait()

    lane_head = lax.broadcasted_iota(jnp.int32, (1, inner), 1) // head_dim
    contract = (((1,), (1,)), ((), ()))

    def attend(c):
        first = (c * step) // seq * seq
        keys_at = pl.ds(pl.multiple_of(first, seq), seq)
        bias_at = pl.ds(pl.multiple_of(c * step - first, step), step)
        q = qkv[0, rows_at(c), :]
        k = qkv[1, keys_at, :]
        v = qkv[2, keys_at, :]
        context = jnp.zeros((step, inner), F32)
        for h in range(heads):
            qh = jnp.where(lane_head == h, q, jnp.zeros_like(q))
            scores = lax.dot_general(qh, k, contract, preferred_element_type=F32)
            scores = scores + bias_v[h, bias_at, :].astype(F32)
            weights = jnp.exp(scores - jnp.max(scores, axis=1, keepdims=True))
            scale = 1.0 / jnp.sum(weights, axis=1, keepdims=True)
            mixed = jnp.dot(weights.astype(BF16), v, preferred_element_type=F32)
            context = jnp.where(lane_head == h, mixed * scale, context)
        ctx_buf[rows_at(c), :] = context.astype(BF16)
        pl.when(is_end)(lambda: ctx_copy(c).start())

    loop(chunks, attend)

    def project_out(context, ref, s):
        block = feats_at(s)
        if wide:
            return jnp.dot(context, ref[:, block], preferred_element_type=F32)
        return lax.dot_general(context, ref[block, :], contract, preferred_element_type=F32)

    def send_out(s, c, up, value):
        out_buf[s, rows_at(c), :] = value.astype(BF16)
        rs_copy(s, c, up).start()

    def own_share(s):
        part[s] = project_out(ctx_buf[...], wo_all, s)

    def originate(c):
        ctx_copy(c).wait_recv()
        context = ctx_in[rows_at(c), :]

        def far(k):
            s = jnp.where(me == 1, n - 1 - k, k)
            value = part[s, rows_at(c), :] + project_out(context, wo_end, s)
            send_out(s, c, jnp.where(me == 1, 1, 0), value)

        def near(k):
            s = jnp.where(me == 1, k, n - 2 + k)
            part[s, rows_at(c), :] += project_out(context, wo_end, s)

        loop(n - 2, far)
        loop(2, near)

    def finished(s, c):
        value = x_all[s, rows_at(c), :].astype(F32) + part[s, rows_at(c), :]
        stream = value.astype(BF16)
        wide_stream = stream.astype(F32)
        return stream, wide_stream * wide_stream

    def finalize(c):
        stream, squares = finished(me, c)
        stream_o[rows_at(c), :] = stream
        part[me, rows_at(c), :] = squares

        @pl.when(is_edge)
        def _():
            end, up = jnp.where(me == 1, 0, n - 1), jnp.where(me == 1, 0, 1)
            stream_end, squares_end = finished(end, c)
            out_buf[end, rows_at(c), :] = stream_end
            rs_copy(end, c, up).start()
            part[me, rows_at(c), :] += squares_end

        total = jnp.sum(part[me, rows_at(c), :], axis=1, keepdims=True)
        turned = jnp.transpose(jnp.broadcast_to(total, (step, 128)))
        ss_mine[c] = turned[0:8, :]
        ss_all[me, c] = turned[0:8, :]
        loop(n, lambda k: ss_copy(me, c, peer_mp(k)).start(), 1)

    def combine(c):
        def message(k):
            for up in (1, 0):
                s = n - 1 - k if up else k
                follows = (me >= 2) if up else (me <= n - 3)
                further = (s > me) if up else (s < me)
                last = (me == n - 2) if up else (me == 1)

                @pl.when(follows & (further | (s == me)))
                def _():
                    rs_copy(s, c, up).wait_recv()
                    value = part[s, rows_at(c), :] + landed[up, s, rows_at(c), :].astype(F32)

                    @pl.when((s == me) | last)
                    def _():
                        part[s, rows_at(c), :] = value

                    @pl.when((s != me) & jnp.logical_not(last))
                    def _():
                        send_out(s, c, up, value)

        loop(n - 2, message)
        finalize(c)

    @pl.when(jnp.logical_not(is_end))
    def _():
        forward_weights(1)
        pl.when(is_edge)(lambda: forward_weights(2))
        other_weights(1)
        pl.when(is_edge)(lambda: other_weights(2))
        loop(n, own_share)
        pl.when(is_edge)(lambda: loop(chunks, originate))
        loop(chunks, combine)

    gain = post_v[...].astype(F32).reshape(1, feats)

    def normalize(c):
        def arrived(s):
            pl.when(s != me)(lambda: ss_copy(s, c, s).wait_recv())

        loop(n - 1, arrived, 1)

        @pl.when(is_end)
        def _():
            up = jnp.where(me == 0, 0, 1)
            rs_copy(me, c, up).wait_recv()
            stream_o[rows_at(c), :] = landed[up, me, rows_at(c), :]

        total = jnp.zeros((8, step), F32)
        for s in range(1, n - 1):
            total = total + ss_all[s, c]
        scale = jnp.transpose(lax.rsqrt(total / model + epsilon))[:, 0:1]
        stream = stream_o[rows_at(c), :].astype(F32)
        normed_o[rows_at(c), :] = (stream * scale * gain).astype(BF16)

    loop(chunks, normalize)

    loop(n, lambda k: gain_copy(me, peer_mp(k)).wait_send(), 1)

    def drain_tokens(s):
        def one(c):
            waited = (odd == 0) & (s == me) & (c < early)

            @pl.when((s <= me) & (me < n - 1) & jnp.logical_not(waited & (me == 0)))
            def _():
                tok_copy(s, c, 1).wait_send()

            @pl.when((s >= me) & (me > 0) & jnp.logical_not(waited & (me == n - 1)))
            def _():
                tok_copy(s, c, 0).wait_send()

            @pl.when(jnp.logical_not(is_end) & (s != me))
            def _():
                rs_copy(s, c, 1).wait_send()
                ss_copy(me, c, s).wait_send()

        loop(chunks, one)

    loop(n, drain_tokens)

    def drain_weights(which):
        weight_copy(which, d, partner, False).wait_send()

        def drain(k):
            weight_copy(which, d, same_core(k), False).wait_send()
            weight_copy(which, from_core(k), partner, True).wait_send()

        loop(half, drain, 1)

    drain_weights(0)
    pl.when(is_edge)(lambda: drain_weights(2))

    @pl.when(is_end)
    def _():
        cross_copy().wait_send()
        loop(chunks, lambda c: ctx_copy(c).wait_send())

    pl.when(jnp.logical_not(is_end))(lambda: drain_weights(1))


def publish(stream_i, normed_i, stream_o, normed_o, sems):
    copies = (
        pltpu.make_async_copy(stream_i, stream_o, sems.at[0]),
        pltpu.make_async_copy(normed_i, normed_o, sems.at[1]),
    )
    for copy in copies:
        copy.start()
    for copy in copies:
        copy.wait()


def on_device(n, groups, tokens, pre_gain, input_weight, output_weight, position_bias, post_gain):
    rows, feats = tokens.shape
    step = 128
    chunks = rows // step
    inner = input_weight.shape[2]
    model = n * feats
    wide = output_weight.shape[1] % 128 == 0
    if not wide:
        output_weight = output_weight.T
    dma, any_space = pltpu.SemaphoreType.DMA, pl.BlockSpec(memory_space=pl.ANY)
    vmem = pl.BlockSpec(memory_space=pltpu.VMEM)
    wo_shape = (inner, model) if wide else (model, inner)
    stream, normed = pl.pallas_call(
        functools.partial(kernel, n, groups, chunks, wide),
        out_shape=(pltpu.VMEM((rows, feats), BF16), pltpu.VMEM((rows, feats), BF16)),
        in_specs=[any_space] * 6,
        out_specs=[vmem] * 2,
        scratch_shapes=[
            pltpu.VMEM((n, rows, feats), BF16),
            pltpu.VMEM((n * feats,), BF16),
            pltpu.VMEM((feats,), BF16),
            pltpu.VMEM((3, model, inner), BF16),
            pltpu.VMEM(wo_shape, BF16),
            pltpu.VMEM(wo_shape, BF16),
            pltpu.VMEM(position_bias.shape, BF16),
            pltpu.VMEM((3, rows, inner), F32),
            pltpu.VMEM((rows, feats), F32),
            pltpu.VMEM((3, rows, inner), BF16),
            pltpu.VMEM((n, rows, feats), F32),
            pltpu.VMEM((n, rows, feats), BF16),
            pltpu.VMEM((2, n, rows, feats), BF16),
            pltpu.VMEM((rows, inner), BF16),
            pltpu.VMEM((rows, inner), BF16),
            pltpu.VMEM((chunks, 8, step), F32),
            pltpu.VMEM((n, chunks, 8, step), F32),
            dma((2, n, chunks)),
            dma((n, chunks)),
            dma((n,)),
            dma((n,)),
            dma((3, 2, groups)),
            dma((3, groups)),
            dma((chunks,)),
            dma((chunks,)),
            dma((n, chunks)),
            dma((2, n, chunks)),
            dma((n, chunks)),
            dma((n, chunks)),
            dma((6,)),
            pltpu.SemaphoreType.REGULAR((2,)),
        ],
        compiler_params=pltpu.CompilerParams(
            collective_id=0, has_side_effects=True, vmem_limit_bytes=56 * 1024 * 1024
        ),
    )(tokens, pre_gain, input_weight, output_weight, position_bias, post_gain)
    shape = jax.ShapeDtypeStruct((rows, feats), BF16)
    return pl.pallas_call(
        publish,
        out_shape=(shape, shape),
        in_specs=[vmem] * 2,
        out_specs=[any_space] * 2,
        scratch_shapes=[dma((2,))],
        compiler_params=pltpu.CompilerParams(vmem_limit_bytes=4 * 1024 * 1024),
    )(stream, normed)


def solution(mesh):
    return jax.shard_map(
        functools.partial(on_device, mesh.shape["mp"], mesh.shape["dp"]),
        mesh=mesh,
        in_specs=(
            P("dp", "mp"),
            P("mp"),
            P(None, "dp", "mp"),
            P("mp", "dp"),
            P("mp", None, None),
            P("mp"),
        ),
        out_specs=(P("dp", "mp"), P("dp", "mp")),
        check_vma=False,
    )
```

time: 54.6 us -> 49.3 us (0.903)
  Pallas kernels: 53.8 us -> 48.5 us
    pallas_call x2, Pallas kernels: 53.8 us -> 48.5 us  [the longest x1 47.7 us: on_device(): pl.pallas_call(functools.partial(kernel, n, groups, chunks, wide), out_sh...]
where the time goes in v2:
time: 49.3 us; the launch traced here: 49.2 us
  Pallas kernels  48.5 us (98%)
  between operations  0.64 us (1%)
    pallas_call x1, Pallas kernels, on_device(): pl.pallas_call(functools.partial(kernel, n, groups, chunks, wide), out_sh...  47.7 us

profile of v2, /device:TPU:1, one launch (start us, length us, event | category | flops | bytes accessed | tf_op | source)
XLA Modules:
  0.0 49.2 jit_solution(1142902010305689544)
XLA Ops:
  0.6 47.7 %shard_map.77 = (bf16[512,256]{1,0:T(8,128)(2,1)S(1)}, bf16[512,256]{1,0:T(8,128)(2,1)S(1)}) custom-call(bf16[512,256]{1,0:T(8,128)(2,1)} %tok.1, bf16[256]{0:T(256)(128)(2,1)} %pre.1, bf16[3,128,256]{2,1,0:T(8,128)(2,1)} %win.1, bf16[256,128]{1,0:T(8,128)(2,1)} %wout.1, bf16[4,512,512]{2,1,0:T(8,128)(2,1)} %bias.1, bf16[256]{0:T(256)(128)(2,1)} %post.1), custom_call_target="tpu_custom_call" | custom-call | tf_op jit(solution)/shard_map/pallas_call | solution.py:534
  48.4 0.8 %shard_map.78 = (bf16[512,256]{1,0:T(8,128)(2,1)}, bf16[512,256]{1,0:T(8,128)(2,1)}) custom-call(bf16[512,256]{1,0:T(8,128)(2,1)S(1)} %get-tuple-element.4.stream_i, bf16[512,256]{1,0:T(8,128)(2,1)S(1)} %get-tuple-element.5.normed_i), custom_call_target="tpu_custom_call" | custom-call | tf_op jit(solution)/shard_map/pallas_call | solution.py:577

commit v3 on v2

--- a/solution.py
+++ b/solution.py
@@ -200,8 +200,6 @@
                 link_free.at[up], inc=1, device_id={"dp": partner}, device_id_type=MESH
             )
 
-    early = max(chunks - 2, 0)
-
     def send_weights(which):
         weight_copy(which, d, partner, False).start()
         loop(half, lambda k: weight_copy(which, d, same_core(k), False).start(), 1)
@@ -222,6 +220,10 @@
         def _():
             weight_copy(2, d, partner, False).wait_recv()
             send_weights(2)
+
+    def forward_out_weights():
+        pl.when(jnp.logical_not(is_end))(lambda: forward_weights(1))
+        pl.when(is_edge)(lambda: forward_weights(2))
 
     def take(up, j, use=None):
         s = me - j if up else me + j
@@ -248,78 +250,16 @@
         for m in range(3):
             acc[m, at, :] += jnp.dot(xg, w_all[m, feats_at(s), :], preferred_element_type=F32)
 
-    def gather_even():
-        send_own(1)
-        send_own(0)
-        send_weights(0)
-        pl.when(is_end)(lambda: cross_copy().start())
-        pl.when(jnp.logical_not(is_end))(lambda: send_weights(1))
-
-        @pl.when(me == 0)
-        def _():
-            loop(early, lambda c: tok_copy(me, c, 1).wait_send())
-            release(1)
-
-        @pl.when(me == n - 1)
-        def _():
-            loop(early, lambda c: tok_copy(me, c, 0).wait_send())
-            release(0)
-
-        def hop(j):
-            def one(c):
-                for up in (1, 0):
-                    s = me - j if up else me + j
-
-                    @pl.when((s >= 0) & (s < n))
-                    def _():
-                        tok_copy(s, c, up).wait_recv()
-                        pl.when(can_send(up))(lambda: tok_copy(s, c, up).start())
-
-            loop(chunks, one)
-            pl.when(j == me)(lambda: release(1))
-            pl.when(j == n - 1 - me)(lambda: release(0))
-
-        loop(n, hop, 1)
-        pass_end_weights()
-        forward_weights(0)
-        loop(n, lambda k: gain_copy(peer_mp(k), peer_mp(k)).wait_recv(), 1)
-        other_weights(0)
-        loop(n, lambda s: accumulate(s, all_rows))
-
-    def gather_odd():
-        send_weights(0)
-        pl.when(is_end)(lambda: cross_copy().start())
-        pl.when(jnp.logical_not(is_end))(lambda: send_weights(1))
-
-        def toward(near):
-            far = 1 - near
-            send_own(near)
-            loop(n, lambda j: take(near, j), 1)
-            pass_end_weights()
-            send_own(far)
-            forward_weights(0)
-            loop(n, lambda k: gain_copy(peer_mp(k), peer_mp(k)).wait_recv(), 1)
-            take(far, 1)
-            other_weights(0)
-
-            def known(s):
-                pl.when((s <= me + 1) if near else (s >= me - 1))(lambda: accumulate(s, all_rows))
-
-            loop(n, known)
-
-            def later(j):
-                take(far, j)
-                s = me + j if near else me - j
-                pl.when((s >= 0) & (s < n))(lambda: accumulate(s, all_rows))
-
-            loop(n, later, 2)
-
-        pl.when(2 * me < n)(lambda: toward(1))
-        pl.when(2 * me >= n)(lambda: toward(0))
-
-    loop(n, lambda k: gain_copy(me, peer_mp(k)).start(), 1)
-    pl.when(odd == 0)(gather_even)
-    pl.when(odd == 1)(gather_odd)
+    def both_ways(action):
+        @pl.when(2 * me < n)
+        def _():
+            action(0)
+            action(1)
+
+        @pl.when(2 * me >= n)
+        def _():
+            action(1)
+            action(0)
 
     def finish(c):
         total = jnp.sum(square[rows_at(c), :], axis=1, keepdims=True)
@@ -327,7 +267,88 @@
         for m in range(3):
             qkv[m, rows_at(c), :] = (acc[m, rows_at(c), :] * inverse).astype(BF16)
 
-    loop(chunks, finish)
+    def send_all_weights():
+        send_weights(0)
+        pl.when(is_end)(lambda: cross_copy().start())
+        pl.when(jnp.logical_not(is_end))(lambda: send_weights(1))
+
+    def wait_gains():
+        loop(n, lambda k: gain_copy(peer_mp(k), peer_mp(k)).wait_recv(), 1)
+
+    def gather_even():
+        both_ways(send_own)
+        send_all_weights()
+
+        @pl.when(is_end)
+        def _():
+            up = jnp.where(me == 0, 1, 0)
+            loop(chunks, lambda c: tok_copy(me, c, up).wait_send())
+            both_ways(release)
+
+        def hop(j):
+            def one(c):
+                def side(up):
+                    s = me - j if up else me + j
+
+                    @pl.when((s >= 0) & (s < n))
+                    def _():
+                        tok_copy(s, c, up).wait_recv()
+                        pl.when(can_send(up))(lambda: tok_copy(s, c, up).start())
+
+                both_ways(side)
+
+            loop(chunks, one)
+
+        loop(n, hop, 1)
+        pl.when(jnp.logical_not(is_end))(lambda: both_ways(release))
+        pass_end_weights()
+        forward_weights(0)
+        wait_gains()
+        other_weights(0)
+        loop(n, lambda s: accumulate(s, all_rows))
+        loop(chunks, finish)
+
+    def gather_odd():
+        send_all_weights()
+        both_ways(send_own)
+
+        def toward(near):
+            far = 1 - near
+            reach = n - 1 - me if near else me
+            loop(n, lambda j: take(near, j), 1)
+            pass_end_weights()
+            forward_weights(0)
+            wait_gains()
+            take(far, 1)
+            other_weights(0)
+
+            def known(s):
+                pl.when((s <= me + 1) if near else (s >= me - 1))(lambda: accumulate(s, all_rows))
+
+            loop(n, known)
+
+            def later(j):
+                @pl.when(j < reach)
+                def _():
+                    take(far, j)
+                    accumulate(me + j if near else me - j, all_rows)
+
+            def use(s, c):
+                accumulate(s, rows_at(c))
+                finish(c)
+
+            loop(n, later, 2)
+            pl.when(reach > 1)(lambda: take(far, reach, use))
+            pl.when(reach <= 1)(lambda: loop(chunks, finish))
+
+        pl.when(2 * me < n)(lambda: toward(1))
+        pl.when(2 * me >= n)(lambda: toward(0))
+        forward_out_weights()
+
+    loop(n, lambda k: gain_copy(me, peer_mp(k)).start(), 1)
+    pl.when(odd == 0)(gather_even)
+    pl.when(odd == 1)(gather_odd)
+
     local[5].wait()
 
     lane_head = lax.broadcasted_iota(jnp.int32, (1, inner), 1) // head_dim
@@ -340,15 +361,15 @@
         q = qkv[0, rows_at(c), :]
         k = qkv[1, keys_at, :]
         v = qkv[2, keys_at, :]
-        context = jnp.zeros((step, inner), F32)
-        for h in range(heads):
-            qh = jnp.where(lane_head == h, q, jnp.zeros_like(q))
-            scores = lax.dot_general(qh, k, contract, preferred_element_type=F32)
-            scores = scores + bias_v[h, bias_at, :].astype(F32)
-            weights = jnp.exp(scores - jnp.max(scores, axis=1, keepdims=True))
-            scale = 1.0 / jnp.sum(weights, axis=1, keepdims=True)
-            mixed = jnp.dot(weights.astype(BF16), v, preferred_element_type=F32)
-            context = jnp.where(lane_head == h, mixed * scale, context)
+        stacked = jnp.concatenate([jnp.where(lane_head == h, q, jnp.zeros_like(q)) for h in range(heads)], axis=0)
+        scores = lax.dot_general(stacked, k, contract, preferred_element_type=F32)
+        scores = scores + bias_v[:, bias_at, :].reshape(heads * step, seq).astype(F32)
+        weights = jnp.exp(scores - jnp.max(scores, axis=1, keepdims=True))
+        scale = 1.0 / jnp.sum(weights, axis=1, keepdims=True)
+        mixed = jnp.dot(weights.astype(BF16), v, preferred_element_type=F32) * scale
+        context = mixed[0:step]
+        for h in range(1, heads):
+            context = jnp.where(lane_head == h, mixed[h * step : (h + 1) * step], context)
         ctx_buf[rows_at(c), :] = context.astype(BF16)
         pl.when(is_end)(lambda: ctx_copy(c).start())
 
@@ -434,8 +455,7 @@
 
     @pl.when(jnp.logical_not(is_end))
     def _():
-        forward_weights(1)
-        pl.when(is_edge)(lambda: forward_weights(2))
+        pl.when(odd == 0)(forward_out_weights)
         other_weights(1)
         pl.when(is_edge)(lambda: other_weights(2))
         loop(n, own_share)
@@ -469,13 +489,13 @@
 
     def drain_tokens(s):
         def one(c):
-            waited = (odd == 0) & (s == me) & (c < early)
-
-            @pl.when((s <= me) & (me < n - 1) & jnp.logical_not(waited & (me == 0)))
+            waited = (odd == 0) & (s == me) & is_end
+
+            @pl.when((s <= me) & (me < n - 1) & jnp.logical_not(waited))
             def _():
                 tok_copy(s, c, 1).wait_send()
 
-            @pl.when((s >= me) & (me > 0) & jnp.logical_not(waited & (me == n - 1)))
+            @pl.when((s >= me) & (me > 0) & jnp.logical_not(waited))
             def _():
                 tok_copy(s, c, 0).wait_send()
 

time: 49.3 us -> 44.9 us (0.911)
  Pallas kernels: 48.5 us -> 44.1 us
    pallas_call x1, Pallas kernels: 47.7 us -> 43.3 us  [on_device(): pl.pallas_call(functools.partial(kernel, n, groups, chunks, wide), out_sh...]
where the time goes in v3:
time: 44.9 us; the launch traced here: 44.8 us
  Pallas kernels  44.1 us (98%)
  between operations  0.64 us (1%)
    pallas_call x1, Pallas kernels, on_device(): pl.pallas_call(functools.partial(kernel, n, groups, chunks, wide), out_sh...  43.3 us

profile of v3, /device:TPU:1, one launch (start us, length us, event | category | flops | bytes accessed | tf_op | source)
XLA Modules:
  0.0 44.8 jit_solution(6015969599908848210)
XLA Ops:
  0.6 43.3 %shard_map.77 = (bf16[512,256]{1,0:T(8,128)(2,1)S(1)}, bf16[512,256]{1,0:T(8,128)(2,1)S(1)}) custom-call(bf16[512,256]{1,0:T(8,128)(2,1)} %tok.1, bf16[256]{0:T(256)(128)(2,1)} %pre.1, bf16[3,128,256]{2,1,0:T(8,128)(2,1)} %win.1, bf16[256,128]{1,0:T(8,128)(2,1)} %wout.1, bf16[4,512,512]{2,1,0:T(8,128)(2,1)} %bias.1, bf16[256]{0:T(256)(128)(2,1)} %post.1), custom_call_target="tpu_custom_call" | custom-call | tf_op jit(solution)/shard_map/pallas_call | solution.py:554
  44.0 0.8 %shard_map.78 = (bf16[512,256]{1,0:T(8,128)(2,1)}, bf16[512,256]{1,0:T(8,128)(2,1)}) custom-call(bf16[512,256]{1,0:T(8,128)(2,1)S(1)} %get-tuple-element.4.stream_i, bf16[512,256]{1,0:T(8,128)(2,1)S(1)} %get-tuple-element.5.normed_i), custom_call_target="tpu_custom_call" | custom-call | tf_op jit(solution)/shard_map/pallas_call | solution.py:597

commit v4 on v3

--- a/solution.py
+++ b/solution.py
@@ -528,6 +528,555 @@
     pl.when(jnp.logical_not(is_end))(lambda: drain_weights(1))
 
 
+def line_kernel(
+    n,
+    groups,
+    chunks,
+    tok,
+    pre,
+    win,
+    wout,
+    bias,
+    post,
+    stream_o,
+    normed_o,
+    x_all,
+    gain_all,
+    post_v,
+    w_all,
+    wo_own,
+    wo_all,
+    bias_v,
+    acc,
+    square,
+    qkv,
+    ctx_all,
+    part,
+    out_buf,
+    landed,
+    ss_mine,
+    ss_all,
+    ag_send,
+    ag_recv,
+    g_send,
+    g_recv,
+    w_send,
+    w_recv,
+    x_send,
+    o_send,
+    o_recv,
+    ctx_send,
+    ctx_recv,
+    end_send,
+    end_recv,
+    ss_send,
+    ss_recv,
+    local_sem,
+    link_free,
+):
+    rows, feats = tok.shape
+    step = rows // chunks
+    pieces = ag_recv.shape[1]
+    piece = rows // pieces
+    heads, seq = bias.shape[0], bias.shape[1]
+    inner = win.shape[2]
+    head_dim = inner // heads
+    model = n * feats
+    wrows = win.shape[1]
+    wcols = model // groups
+    half = groups // 2
+    me = lax.axis_index("mp")
+    d = lax.axis_index("dp")
+    odd = lax.rem(d, 2)
+    pair = d // 2
+    partner = d + 1 - 2 * odd
+    low = 2 * me < n
+    is_end = (me == 0) | (me == n - 1)
+    is_inner = jnp.logical_not(is_end)
+    near_end, far_end = jnp.where(low, 0, n - 1), jnp.where(low, n - 1, 0)
+    other_inner = n - 1 - me
+    inwards = me + jnp.where(low, 1, -1)
+    home = jnp.where(d < half, 1, n - 2)
+    is_source = me == home
+    all_rows = pl.ds(0, rows)
+
+    def rows_at(c):
+        return pl.ds(pl.multiple_of(c * step, step), step)
+
+    def feats_at(s):
+        return pl.ds(pl.multiple_of(s * feats, feats), feats)
+
+    def loop(count, body, start=0):
+        def wrapped(i, carry):
+            body(i)
+            return carry
+
+        lax.fori_loop(start, count, wrapped, 0)
+
+    def remote(src, dst, send, recv, target):
+        return pltpu.make_async_remote_copy(
+            src_ref=src,
+            dst_ref=dst,
+            send_sem=send,
+            recv_sem=recv,
+            device_id=target,
+            device_id_type=MESH,
+        )
+
+    def tok_copy(s, c, up):
+        ref = x_all.at[s, pl.ds(pl.multiple_of(c * piece, piece), piece)]
+        return remote(ref, ref, ag_send.at[up, s, c], ag_recv.at[s, c], {"mp": me + 2 * up - 1})
+
+    def gain_copy(origin, target):
+        ref = gain_all.at[feats_at(origin)]
+        return remote(ref, ref, g_send.at[target], g_recv.at[origin], {"mp": target})
+
+    def w_slot(o):
+        return w_all.at[:, pl.ds(pl.multiple_of(o * wrows, wrows), wrows), :]
+
+    def w_copy(o, target, forward):
+        send = w_send.at[1, o] if forward else w_send.at[0, target]
+        return remote(w_slot(o), w_slot(o), send, w_recv.at[o], {"dp": target})
+
+    def o_slot(z, o):
+        return wo_all.at[z, :, pl.ds(pl.multiple_of(lax.rem(o, half) * wcols, wcols), wcols)]
+
+    def o_copy(z, o, target, forward):
+        send = o_send.at[1, z, o] if forward else o_send.at[0, z, target]
+        return remote(o_slot(z, o), o_slot(z, o), send, o_recv.at[z, o], {"dp": target})
+
+    def cross_copy():
+        return remote(wo_own, o_slot(me, d), x_send.at[0], o_recv.at[me, d], {"mp": home})
+
+    def ctx_copy(s, c):
+        ref = ctx_all.at[s, rows_at(c)]
+        return remote(ref, ref, ctx_send.at[s, c], ctx_recv.at[s, c], {"mp": inwards})
+
+    def end_copy(c):
+        return remote(
+            out_buf.at[rows_at(c)], landed.at[rows_at(c)], end_send.at[c], end_recv.at[c], {"mp": near_end}
+        )
+
+    def ss_copy(origin, c, target):
+        return remote(
+            ss_mine.at[c], ss_all.at[origin, c], ss_send.at[target, c], ss_recv.at[origin, c], {"mp": target}
+        )
+
+    tok_in = pltpu.make_async_copy(tok, x_all.at[me], local_sem.at[0])
+    win_in = pltpu.make_async_copy(win, w_slot(d), local_sem.at[1])
+    pre_in = pltpu.make_async_copy(pre, gain_all.at[feats_at(me)], local_sem.at[2])
+    post_in = pltpu.make_async_copy(post, post_v, local_sem.at[3])
+    bias_in = pltpu.make_async_copy(bias, bias_v, local_sem.at[4])
+
+    def wout_in(action):
+        pl.when(is_source)(lambda: action(pltpu.make_async_copy(wout, o_slot(me, d), local_sem.at[5])))
+        pl.when(jnp.logical_not(is_source))(
+            lambda: action(pltpu.make_async_copy(wout, wo_own, local_sem.at[5]))
+        )
+
+    tok_in.start()
+    win_in.start()
+    pre_in.start()
+    wout_in(lambda copy: copy.start())
+    post_in.start()
+    bias_in.start()
+
+    def peer_mp(k):
+        return lax.rem(me + k, n)
+
+    def same_core(k):
+        return 2 * lax.rem(pair + k, half) + odd
+
+    def from_core(k):
+        return 2 * lax.rem(pair + half - k, half) + odd
+
+    barrier = pltpu.get_barrier_semaphore()
+
+    def greet(target):
+        pl.semaphore_signal(barrier, inc=1, device_id=target, device_id_type=MESH)
+
+    loop(n, lambda k: greet({"mp": peer_mp(k)}), 1)
+    loop(half, lambda k: greet({"dp": same_core(k)}), 1)
+    greet({"dp": partner})
+    acc[...] = jnp.zeros_like(acc)
+    square[...] = jnp.zeros_like(square)
+    tok_in.wait()
+    pl.semaphore_wait(barrier, n - 1 + half - 1 + 1)
+
+    def can_send(up):
+        return (me < n - 1) if up else (me > 0)
+
+    def send_own(up):
+        @pl.when(can_send(up))
+        def _():
+            @pl.when(odd == 1)
+            def _():
+                pl.semaphore_wait(link_free.at[up], 1)
+
+            loop(pieces, lambda c: tok_copy(me, c, up).start())
+
+    def release(up):
+        @pl.when(can_send(up))
+        def _():
+            pl.semaphore_signal(
+                link_free.at[up], inc=1, device_id={"dp": partner}, device_id_type=MESH
+            )
+
+    def both_ways(action):
+        @pl.when(low)
+        def _():
+            action(0)
+            action(1)
+
+        @pl.when(jnp.logical_not(low))
+        def _():
+            action(1)
+            action(0)
+
+    def in_plane(o):
+        return (o < half) == (me == 1)
+
+    def send_slice(z):
+        o_copy(z, d, partner, False).start()
+        loop(half, lambda k: o_copy(z, d, same_core(k), False).start(), 1)
+
+    def relay_slice(z):
+        @pl.when(is_source)
+        def _():
+            o_copy(z, d, partner, False).wait_recv()
+            send_slice(z)
+
+    def forward_slices(z):
+        def forward(k):
+            o = from_core(k)
+
+            @pl.when(in_plane(o))
+            def _():
+                o_copy(z, o, partner, False).wait_recv()
+                o_copy(z, o, partner, True).start()
+
+        loop(half, forward, 1)
+
+    def other_slices(z):
+        def other(k):
+            o = 2 * k + 1 - odd
+            pl.when(in_plane(o))(lambda: o_copy(z, o, partner, False).wait_recv())
+
+        loop(half, other)
+
+    def send_weights():
+        win_in.wait()
+        w_copy(d, partner, False).start()
+        loop(half, lambda k: w_copy(d, same_core(k), False).start(), 1)
+        pre_in.wait()
+        loop(n, lambda k: gain_copy(me, peer_mp(k)).start(), 1)
+        wout_in(lambda copy: copy.wait())
+        pl.when(is_source)(lambda: send_slice(me))
+
+    def send_cross():
+        pl.when(jnp.logical_not(is_source))(lambda: cross_copy().start())
+
+    def forward_weights():
+        def forward(k):
+            o = from_core(k)
+            w_copy(o, partner, False).wait_recv()
+            w_copy(o, partner, True).start()
+
+        loop(half, forward, 1)
+        loop(n, lambda k: gain_copy(peer_mp(k), peer_mp(k)).wait_recv(), 1)
+
+    def other_weights():
+        loop(half, lambda k: w_copy(2 * k + 1 - odd, partner, False).wait_recv())
+
+    def take(up, j, use=None):
+        s = me - j if up else me + j
+
+        @pl.when((s >= 0) & (s < n))
+        def _():
+            def one(c):
+                tok_copy(s, c, up).wait_recv()
+                pl.when(can_send(up))(lambda: tok_copy(s, c, up).start())
+
+            if use is None:
+                loop(pieces, one)
+            else:
+                per = pieces // chunks
+
+                def block(c):
+                    loop(per, lambda i: one(c * per + i))
+                    use(s, c)
+
+                loop(chunks, block)
+
+    def accumulate(s, at):
+        gain = gain_all[feats_at(s)].astype(F32).reshape(1, feats)
+        x = x_all[s, at, :].astype(F32)
+        square[at, :] += x * x
+        xg = (x * gain).astype(BF16)
+        for m in range(3):
+            acc[m, at, :] += jnp.dot(xg, w_all[m, feats_at(s), :], preferred_element_type=F32)
+
+    def finish(c):
+        total = jnp.sum(square[rows_at(c), :], axis=1, keepdims=True)
+        inverse = lax.rsqrt(total / model + epsilon)
+        for m in range(3):
+            qkv[m, rows_at(c), :] = (acc[m, rows_at(c), :] * inverse).astype(BF16)
+
+    def gather_by_shard(near):
+        far = 1 - near
+        reach = n - 1 - me if near else me
+        loop(n, lambda j: take(near, j), 1)
+        pl.when(odd == 1)(send_cross)
+        forward_weights()
+        relay_slice(near_end)
+        relay_slice(far_end)
+        take(far, 1)
+        other_weights()
+
+        def known(s):
+            pl.when((s <= me + 1) if near else (s >= me - 1))(lambda: accumulate(s, all_rows))
+
+        loop(n, known)
+
+        def later(j):
+            @pl.when(j < reach)
+            def _():
+                take(far, j)
+                accumulate(me + j if near else me - j, all_rows)
+
+        def use(s, c):
+            accumulate(s, rows_at(c))
+            finish(c)
+
+        loop(n, later, 2)
+        take(far, reach, use)
+        relay_slice(other_inner)
+
+    def by_shard():
+        pl.when(low)(lambda: gather_by_shard(1))
+        pl.when(jnp.logical_not(low))(lambda: gather_by_shard(0))
+
+    def gather_even():
+        both_ways(send_own)
+        send_weights()
+
+        @pl.when(is_end)
+        def _():
+            up = jnp.where(me == 0, 1, 0)
+            loop(pieces, lambda c: tok_copy(me, c, up).wait_send())
+            both_ways(release)
+            send_cross()
+            by_shard()
+
+        def hop(j):
+            def one(c):
+                def side(up):
+                    s = me - j if up else me + j
+
+                    @pl.when((s >= 0) & (s < n))
+                    def _():
+                        tok_copy(s, c, up).wait_recv()
+                        pl.when(can_send(up))(lambda: tok_copy(s, c, up).start())
+
+                both_ways(side)
+
+            loop(pieces, one)
+
+        @pl.when(is_inner)
+        def _():
+            hop(1)
+            pl.when(low)(lambda: release(0))
+            pl.when(jnp.logical_not(low))(lambda: release(1))
+            loop(n - 1, hop, 2)
+            pl.when(low)(lambda: release(1))
+            pl.when(jnp.logical_not(low))(lambda: release(0))
+            send_cross()
+            forward_weights()
+            relay_slice(near_end)
+            relay_slice(far_end)
+            other_weights()
+            relay_slice(other_inner)
+            loop(n, lambda s: accumulate(s, all_rows))
+            loop(chunks, finish)
+
+    def gather_odd():
+        send_weights()
+        both_ways(send_own)
+        by_shard()
+
+        @pl.when(is_inner)
+        def _():
+            forward_slices(me)
+            forward_slices(near_end)
+            forward_slices(far_end)
+
+    pl.when(odd == 0)(gather_even)
+    pl.when(odd == 1)(gather_odd)
+    post_in.wait()
+    bias_in.wait()
+
+    lane_head = lax.broadcasted_iota(jnp.int32, (1, inner), 1) // head_dim
+    contract = (((1,), (1,)), ((), ()))
+
+    def attend(c):
+        first = (c * step) // seq * seq
+        keys_at = pl.ds(first, seq)
+        bias_at = pl.ds(c * step - first, step)
+        q = qkv[0, rows_at(c), :]
+        k = qkv[1, keys_at, :]
+        v = qkv[2, keys_at, :]
+        stacked = jnp.concatenate([jnp.where(lane_head == h, q, jnp.zeros_like(q)) for h in range(heads)], axis=0)
+        scores = lax.dot_general(stacked, k, contract, preferred_element_type=F32)
+        scores = scores + bias_v[:, bias_at, :].reshape(heads * step, seq).astype(F32)
+        weights = jnp.exp(scores - jnp.max(scores, axis=1, keepdims=True))
+        scale = 1.0 / jnp.sum(weights, axis=1, keepdims=True)
+        mixed = jnp.dot(weights.astype(BF16), v, preferred_element_type=F32) * scale
+        context = mixed[0:step]
+        for h in range(1, heads):
+            context = jnp.where(lane_head == h, mixed[h * step : (h + 1) * step], context)
+        ctx_all[me, rows_at(c), :] = context.astype(BF16)
+
+    for c in range(0, chunks, 2):
+        together = range(c, min(c + 2, chunks))
+        for i in together:
+            attend(i)
+        for i in together:
+            ctx_copy(me, i).start()
+
+    def drain_line(s):
+        @pl.when(s != me)
+        def _():
+            gain_copy(me, s).wait_send()
+
+        def one(c):
+            waited = (odd == 0) & (s == me) & is_end
+
+            @pl.when((s <= me) & (me < n - 1) & jnp.logical_not(waited))
+            def _():
+                tok_copy(s, c, 1).wait_send()
+
+            @pl.when((s >= me) & (me > 0) & jnp.logical_not(waited))
+            def _():
+                tok_copy(s, c, 0).wait_send()
+
+        loop(pieces, one)
+
+        @pl.when(is_source)
+        def _():
+            o_copy(s, d, partner, False).wait_send()
+            loop(half, lambda k: o_copy(s, d, same_core(k), False).wait_send(), 1)
+
+    def drain_early():
+        loop(n, drain_line)
+        w_copy(d, partner, False).wait_send()
+
+        def drain_weights(k):
+            w_copy(d, same_core(k), False).wait_send()
+            w_copy(from_core(k), partner, True).wait_send()
+
+        loop(half, drain_weights, 1)
+        pl.when(jnp.logical_not(is_source))(lambda: cross_copy().wait_send())
+        loop(chunks, lambda c: ctx_copy(me, c).wait_send())
+
+    def project_out(s, at, first=False):
+        value = jnp.dot(ctx_all[s, at, :], wo_all[s], preferred_element_type=F32)
+        part[at, :] = value if first else part[at, :] + value
+
+    def pass_on(c):
+        ctx_copy(near_end, c).wait_recv()
+        ctx_copy(near_end, c).start()
+
+    def finalize(c):
+        def block(s, at):
+            stream = (x_all[s, rows_at(c), :].astype(F32) + part[rows_at(c), at]).astype(BF16)
+            wide_stream = stream.astype(F32)
+            return stream, wide_stream * wide_stream
+
+        def both(own_at, end_at):
+            stream_end, squares_end = block(near_end, end_at)
+            out_buf[rows_at(c), :] = stream_end
+            end_copy(c).start()
+            stream, squares = block(me, own_at)
+            stream_o[rows_at(c), :] = stream
+            total = jnp.sum(squares + squares_end, axis=1, keepdims=True)
+            turned = jnp.transpose(jnp.broadcast_to(total, (step, 128)))
+            ss_mine[c] = turned[0:8, :]
+            ss_all[me, c] = turned[0:8, :]
+
+        pl.when(low)(lambda: both(pl.ds(feats, feats), pl.ds(0, feats)))
+        pl.when(jnp.logical_not(low))(lambda: both(pl.ds(0, feats), pl.ds(feats, feats)))
+        loop(n, lambda k: ss_copy(me, c, peer_mp(k)).start(), 1)
+
+    pl.when(is_end)(drain_early)
+
+    @pl.when(is_inner)
+    def _():
+        @pl.when(odd == 0)
+        def _():
+            forward_slices(me)
+            forward_slices(near_end)
+
+        pl.when(odd == 1)(lambda: forward_slices(other_inner))
+
+        loop(chunks, pass_on)
+        @pl.when(odd == 0)
+        def _():
+            forward_slices(far_end)
+            forward_slices(other_inner)
+
+        loop(n, other_slices)
+        project_out(me, all_rows, True)
+        drain_early()
+        loop(chunks, lambda c: ctx_copy(other_inner, c).wait_recv())
+        project_out(other_inner, all_rows)
+
+        project_out(near_end, all_rows)
+
+        def last(c):
+            ctx_copy(far_end, c).wait_recv()
+            project_out(far_end, rows_at(c))
+            finalize(c)
+
+        loop(chunks, last)
+
+    gain = post_v[...].astype(F32).reshape(1, feats)
+
+    def normalize(c):
+        def arrived(s):
+            pl.when(s != me)(lambda: ss_copy(s, c, s).wait_recv())
+
+        loop(n - 1, arrived, 1)
+
+        @pl.when(is_end)
+        def _():
+            end_copy(c).wait_recv()
+            stream_o[rows_at(c), :] = landed[rows_at(c), :]
+
+        total = ss_all[1, c] + ss_all[n - 2, c]
+        scale = jnp.transpose(lax.rsqrt(total / model + epsilon))[:, 0:1]
+        stream = stream_o[rows_at(c), :].astype(F32)
+        normed_o[rows_at(c), :] = (stream * scale * gain).astype(BF16)
+
+    loop(chunks, normalize)
+
+    def drain_late(c):
+        ctx_copy(near_end, c).wait_send()
+        end_copy(c).wait_send()
+        loop(n, lambda k: ss_copy(me, c, peer_mp(k)).wait_send(), 1)
+
+    def drain_slices(z):
+        def forwarded(k):
+            o = from_core(k)
+            pl.when(in_plane(o))(lambda: o_copy(z, o, partner, True).wait_send())
+
+        loop(half, forwarded, 1)
+
+    @pl.when(is_inner)
+    def _():
+        loop(chunks, drain_late)
+        loop(n, drain_slices)
+
+
 def publish(stream_i, normed_i, stream_o, normed_o, sems):
     copies = (
         pltpu.make_async_copy(stream_i, stream_o, sems.at[0]),
@@ -550,13 +1099,48 @@
         output_weight = output_weight.T
     dma, any_space = pltpu.SemaphoreType.DMA, pl.BlockSpec(memory_space=pl.ANY)
     vmem = pl.BlockSpec(memory_space=pltpu.VMEM)
-    wo_shape = (inner, model) if wide else (model, inner)
-    stream, normed = pl.pallas_call(
-        functools.partial(kernel, n, groups, chunks, wide),
-        out_shape=(pltpu.VMEM((rows, feats), BF16), pltpu.VMEM((rows, feats), BF16)),
-        in_specs=[any_space] * 6,
-        out_specs=[vmem] * 2,
-        scratch_shapes=[
+    if wide and n - 2 == 2:
+        pieces = rows // 64
+        body = functools.partial(line_kernel, n, groups, chunks)
+        scratch = [
+            pltpu.VMEM((n, rows, feats), BF16),
+            pltpu.VMEM((n * feats,), BF16),
+            pltpu.VMEM((feats,), BF16),
+            pltpu.VMEM((3, model, inner), BF16),
+            pltpu.VMEM(output_weight.shape, BF16),
+            pltpu.VMEM((n, inner, 2 * feats), BF16),
+            pltpu.VMEM(position_bias.shape, BF16),
+            pltpu.VMEM((3, rows, inner), F32),
+            pltpu.VMEM((rows, feats), F32),
+            pltpu.VMEM((3, rows, inner), BF16),
+            pltpu.VMEM((n, rows, inner), BF16),
+            pltpu.VMEM((rows, 2 * feats), F32),
+            pltpu.VMEM((rows, feats), BF16),
+            pltpu.VMEM((rows, feats), BF16),
+            pltpu.VMEM((chunks, 8, step), F32),
+            pltpu.VMEM((n, chunks, 8, step), F32),
+            dma((2, n, pieces)),
+            dma((n, pieces)),
+            dma((n,)),
+            dma((n,)),
+            dma((2, groups)),
+            dma((groups,)),
+            dma((1,)),
+            dma((2, n, groups)),
+            dma((n, groups)),
+            dma((n, chunks)),
+            dma((n, chunks)),
+            dma((chunks,)),
+            dma((chunks,)),
+            dma((n, chunks)),
+            dma((n, chunks)),
+            dma((6,)),
+            pltpu.SemaphoreType.REGULAR((2,)),
+        ]
+    else:
+        body = functools.partial(kernel, n, groups, chunks, wide)
+        wo_shape = (inner, model) if wide else (model, inner)
+        scratch = [
             pltpu.VMEM((n, rows, feats), BF16),
             pltpu.VMEM((n * feats,), BF16),
             pltpu.VMEM((feats,), BF16),
@@ -588,7 +1172,13 @@
             dma((n, chunks)),
             dma((6,)),
             pltpu.SemaphoreType.REGULAR((2,)),
-        ],
+        ]
+    stream, normed = pl.pallas_call(
+        body,
+        out_shape=(pltpu.VMEM((rows, feats), BF16), pltpu.VMEM((rows, feats), BF16)),
+        in_specs=[any_space] * 6,
+        out_specs=[vmem] * 2,
+        scratch_shapes=scratch,
         compiler_params=pltpu.CompilerParams(
             collective_id=0, has_side_effects=True, vmem_limit_bytes=56 * 1024 * 1024
         ),

time: 44.9 us -> 42.6 us (0.949)
  Pallas kernels: 44.1 us -> 41.8 us
    pallas_call x1, Pallas kernels: 43.3 us -> 41 us  [on_device(): pl.pallas_call(body, out_shape=(pltpu.VMEM((rows, feats), BF16), pltpu.VM...]
where the time goes in v4:
time: 42.6 us; the launch traced here: 42.4 us
  Pallas kernels  41.8 us (98%)
  between operations  0.64 us (2%)
    pallas_call x1, Pallas kernels, on_device(): pl.pallas_call(body, out_shape=(pltpu.VMEM((rows, feats), BF16), pltpu.VM...  41 us

profile of v4, /device:TPU:1, one launch (start us, length us, event | category | flops | bytes accessed | tf_op | source)
XLA Modules:
  0.0 42.4 jit_solution(11523060660355054118)
XLA Ops:
  0.6 41.0 %shard_map.77 = (bf16[512,256]{1,0:T(8,128)(2,1)S(1)}, bf16[512,256]{1,0:T(8,128)(2,1)S(1)}) custom-call(bf16[512,256]{1,0:T(8,128)(2,1)} %tok.1, bf16[256]{0:T(256)(128)(2,1)} %pre.1, bf16[3,128,256]{2,1,0:T(8,128)(2,1)} %win.1, bf16[256,128]{1,0:T(8,128)(2,1)} %wout.1, bf16[4,512,512]{2,1,0:T(8,128)(2,1)} %bias.1, bf16[256]{0:T(256)(128)(2,1)} %post.1), custom_call_target="tpu_custom_call" | custom-call | tf_op jit(solution)/shard_map/pallas_call | solution.py:1176
  41.6 0.8 %shard_map.78 = (bf16[512,256]{1,0:T(8,128)(2,1)}, bf16[512,256]{1,0:T(8,128)(2,1)}) custom-call(bf16[512,256]{1,0:T(8,128)(2,1)S(1)} %get-tuple-element.4.stream_i, bf16[512,256]{1,0:T(8,128)(2,1)S(1)} %get-tuple-element.5.normed_i), custom_call_target="tpu_custom_call" | custom-call | tf_op jit(solution)/shard_map/pallas_call | solution.py:1187

commit v5 on v4

--- a/solution.py
+++ b/solution.py
@@ -598,6 +598,7 @@
     inwards = me + jnp.where(low, 1, -1)
     home = jnp.where(d < half, 1, n - 2)
     is_source = me == home
+    late_cross = is_end & (home == inwards) & (odd == 1)
     all_rows = pl.ds(0, rows)
 
     def rows_at(c):
@@ -639,7 +640,7 @@
         return remote(w_slot(o), w_slot(o), send, w_recv.at[o], {"dp": target})
 
     def o_slot(z, o):
-        return wo_all.at[z, :, pl.ds(pl.multiple_of(lax.rem(o, half) * wcols, wcols), wcols)]
+        return wo_all.at[z, lax.rem(o, half)]
 
     def o_copy(z, o, target, forward):
         send = o_send.at[1, z, o] if forward else o_send.at[0, z, target]
@@ -678,8 +679,6 @@
     win_in.start()
     pre_in.start()
     wout_in(lambda copy: copy.start())
-    post_in.start()
-    bias_in.start()
 
     def peer_mp(k):
         return lax.rem(me + k, n)
@@ -701,6 +700,8 @@
     acc[...] = jnp.zeros_like(acc)
     square[...] = jnp.zeros_like(square)
     tok_in.wait()
+    post_in.start()
+    bias_in.start()
     pl.semaphore_wait(barrier, n - 1 + half - 1 + 1)
 
     def can_send(up):
@@ -772,9 +773,7 @@
         loop(n, lambda k: gain_copy(me, peer_mp(k)).start(), 1)
         wout_in(lambda copy: copy.wait())
         pl.when(is_source)(lambda: send_slice(me))
-
-    def send_cross():
-        pl.when(jnp.logical_not(is_source))(lambda: cross_copy().start())
+        pl.when(jnp.logical_not(is_source | late_cross))(lambda: cross_copy().start())
 
     def forward_weights():
         def forward(k):
@@ -826,10 +825,11 @@
         far = 1 - near
         reach = n - 1 - me if near else me
         loop(n, lambda j: take(near, j), 1)
-        pl.when(odd == 1)(send_cross)
+        pl.when(late_cross)(lambda: cross_copy().start())
         forward_weights()
         relay_slice(near_end)
         relay_slice(far_end)
+        relay_slice(other_inner)
         take(far, 1)
         other_weights()
 
@@ -850,7 +850,6 @@
 
         loop(n, later, 2)
         take(far, reach, use)
-        relay_slice(other_inner)
 
     def by_shard():
         pl.when(low)(lambda: gather_by_shard(1))
@@ -865,10 +864,9 @@
             up = jnp.where(me == 0, 1, 0)
             loop(pieces, lambda c: tok_copy(me, c, up).wait_send())
             both_ways(release)
-            send_cross()
             by_shard()
 
-        def hop(j):
+        def hop(j, start=0, stop=pieces):
             def one(c):
                 def side(up):
                     s = me - j if up else me + j
@@ -880,24 +878,25 @@
 
                 both_ways(side)
 
-            loop(pieces, one)
+            loop(stop, one, start)
 
         @pl.when(is_inner)
         def _():
             hop(1)
             pl.when(low)(lambda: release(0))
             pl.when(jnp.logical_not(low))(lambda: release(1))
-            loop(n - 1, hop, 2)
+            hop(2, 0, pieces // 2)
             pl.when(low)(lambda: release(1))
             pl.when(jnp.logical_not(low))(lambda: release(0))
-            send_cross()
+            hop(2, pieces // 2)
             forward_weights()
             relay_slice(near_end)
             relay_slice(far_end)
+            relay_slice(other_inner)
             other_weights()
-            relay_slice(other_inner)
             loop(n, lambda s: accumulate(s, all_rows))
             loop(chunks, finish)
+            forward_slices(me)
 
     def gather_odd():
         send_weights()
@@ -979,7 +978,8 @@
         loop(chunks, lambda c: ctx_copy(me, c).wait_send())
 
     def project_out(s, at, first=False):
-        value = jnp.dot(ctx_all[s, at, :], wo_all[s], preferred_element_type=F32)
+        weight = jnp.concatenate([wo_all[s, i] for i in range(wo_all.shape[1])], axis=1)
+        value = jnp.dot(ctx_all[s, at, :], weight, preferred_element_type=F32)
         part[at, :] = value if first else part[at, :] + value
 
     def pass_on(c):
@@ -1013,24 +1013,24 @@
     def _():
         @pl.when(odd == 0)
         def _():
-            forward_slices(me)
             forward_slices(near_end)
+            forward_slices(far_end)
 
         pl.when(odd == 1)(lambda: forward_slices(other_inner))
-
-        loop(chunks, pass_on)
-        @pl.when(odd == 0)
-        def _():
-            forward_slices(far_end)
-            forward_slices(other_inner)
-
-        loop(n, other_slices)
+        other_slices(me)
         project_out(me, all_rows, True)
-        drain_early()
+        other_slices(near_end)
+        def near(c):
+            pass_on(c)
+            project_out(near_end, rows_at(c))
+
+        loop(chunks // 2, near)
+        pl.when(odd == 0)(lambda: forward_slices(other_inner))
+        loop(chunks, near, chunks // 2)
+        other_slices(other_inner)
         loop(chunks, lambda c: ctx_copy(other_inner, c).wait_recv())
         project_out(other_inner, all_rows)
-
-        project_out(near_end, all_rows)
+        other_slices(far_end)
 
         def last(c):
             ctx_copy(far_end, c).wait_recv()
@@ -1073,6 +1073,7 @@
 
     @pl.when(is_inner)
     def _():
+        drain_early()
         loop(chunks, drain_late)
         loop(n, drain_slices)
 
@@ -1108,7 +1109,7 @@
             pltpu.VMEM((feats,), BF16),
             pltpu.VMEM((3, model, inner), BF16),
             pltpu.VMEM(output_weight.shape, BF16),
-            pltpu.VMEM((n, inner, 2 * feats), BF16),
+            pltpu.VMEM((n, groups // 2, inner, output_weight.shape[1]), BF16),
             pltpu.VMEM(position_bias.shape, BF16),
             pltpu.VMEM((3, rows, inner), F32),
             pltpu.VMEM((rows, feats), F32),

time: 42.6 us -> 41.9 us (0.984)
  Pallas kernels: 41.8 us -> 41.1 us
    pallas_call x1, Pallas kernels: 41 us -> 40.3 us  [on_device(): pl.pallas_call(body, out_shape=(pltpu.VMEM((rows, feats), BF16), pltpu.VM...]
where the time goes in v5:
time: 41.9 us; the launch traced here: 41.7 us
  Pallas kernels  41.1 us (98%)
  between operations  0.64 us (2%)
    pallas_call x1, Pallas kernels, on_device(): pl.pallas_call(body, out_shape=(pltpu.VMEM((rows, feats), BF16), pltpu.VM...  40.3 us

profile of v5, /device:TPU:1, one launch (start us, length us, event | category | flops | bytes accessed | tf_op | source)
XLA Modules:
  0.0 41.7 jit_solution(8051817885780265597)
XLA Ops:
  0.6 40.3 %shard_map.77 = (bf16[512,256]{1,0:T(8,128)(2,1)S(1)}, bf16[512,256]{1,0:T(8,128)(2,1)S(1)}) custom-call(bf16[512,256]{1,0:T(8,128)(2,1)} %tok.1, bf16[256]{0:T(256)(128)(2,1)} %pre.1, bf16[3,128,256]{2,1,0:T(8,128)(2,1)} %win.1, bf16[256,128]{1,0:T(8,128)(2,1)} %wout.1, bf16[4,512,512]{2,1,0:T(8,128)(2,1)} %bias.1, bf16[256]{0:T(256)(128)(2,1)} %post.1), custom_call_target="tpu_custom_call" | custom-call | tf_op jit(solution)/shard_map/pallas_call | solution.py:1177
  40.9 0.8 %shard_map.78 = (bf16[512,256]{1,0:T(8,128)(2,1)}, bf16[512,256]{1,0:T(8,128)(2,1)}) custom-call(bf16[512,256]{1,0:T(8,128)(2,1)S(1)} %get-tuple-element.4.stream_i, bf16[512,256]{1,0:T(8,128)(2,1)S(1)} %get-tuple-element.5.normed_i), custom_call_target="tpu_custom_call" | custom-call | tf_op jit(solution)/shard_map/pallas_call | solution.py:1188

commit v6 on v5

--- a/solution.py
+++ b/solution.py
@@ -626,41 +626,51 @@
 
     def tok_copy(s, c, up):
         ref = x_all.at[s, pl.ds(pl.multiple_of(c * piece, piece), piece)]
-        return remote(ref, ref, ag_send.at[up, s, c], ag_recv.at[s, c], {"mp": me + 2 * up - 1})
+        return remote(ref, ref, ag_send.at[up, s], ag_recv.at[s, c], {"mp": me + 2 * up - 1})
+
+    def sent(ref, sem):
+        remote(ref, ref, sem, ctx_recv.at[0, 0], {"mp": inwards}).wait_send()
+
+    def tokens_sent(s, up):
+        sent(x_all.at[s], ag_send.at[up, s])
 
     def gain_copy(origin, target):
         ref = gain_all.at[feats_at(origin)]
-        return remote(ref, ref, g_send.at[target], g_recv.at[origin], {"mp": target})
+        return remote(ref, ref, g_send.at[0], g_recv.at[0], {"mp": target})
+
+    def all_gains():
+        ref = gain_all.at[pl.ds(0, (n - 1) * feats)]
+        return remote(ref, ref, g_send.at[0], g_recv.at[0], {"mp": inwards})
 
     def w_slot(o):
         return w_all.at[:, pl.ds(pl.multiple_of(o * wrows, wrows), wrows), :]
 
     def w_copy(o, target, forward):
-        send = w_send.at[1, o] if forward else w_send.at[0, target]
+        send = w_send.at[1 if forward else 0]
         return remote(w_slot(o), w_slot(o), send, w_recv.at[o], {"dp": target})
 
     def o_slot(z, o):
         return wo_all.at[z, lax.rem(o, half)]
 
     def o_copy(z, o, target, forward):
-        send = o_send.at[1, z, o] if forward else o_send.at[0, z, target]
-        return remote(o_slot(z, o), o_slot(z, o), send, o_recv.at[z, o], {"dp": target})
+        send = o_send.at[1 if forward else 0, z]
+        return remote(o_slot(z, o), o_slot(z, o), send, o_recv.at[z, lax.rem(o, half)], {"dp": target})
 
     def cross_copy():
-        return remote(wo_own, o_slot(me, d), x_send.at[0], o_recv.at[me, d], {"mp": home})
+        return remote(wo_own, o_slot(me, d), x_send.at[0], o_recv.at[me, lax.rem(d, half)], {"mp": home})
 
     def ctx_copy(s, c):
         ref = ctx_all.at[s, rows_at(c)]
-        return remote(ref, ref, ctx_send.at[s, c], ctx_recv.at[s, c], {"mp": inwards})
+        return remote(ref, ref, ctx_send.at[jnp.where(s == me, 0, 1)], ctx_recv.at[s, c], {"mp": inwards})
 
     def end_copy(c):
         return remote(
-            out_buf.at[rows_at(c)], landed.at[rows_at(c)], end_send.at[c], end_recv.at[c], {"mp": near_end}
+            out_buf.at[rows_at(c)], landed.at[rows_at(c)], end_send.at[0], end_recv.at[c], {"mp": near_end}
         )
 
     def ss_copy(origin, c, target):
         return remote(
-            ss_mine.at[c], ss_all.at[origin, c], ss_send.at[target, c], ss_recv.at[origin, c], {"mp": target}
+            ss_mine.at[c], ss_all.at[origin, c], ss_send.at[0], ss_recv.at[jnp.where(origin == 1, 0, 1), c], {"mp": target}
         )
 
     tok_in = pltpu.make_async_copy(tok, x_all.at[me], local_sem.at[0])
@@ -782,7 +792,7 @@
             w_copy(o, partner, True).start()
 
         loop(half, forward, 1)
-        loop(n, lambda k: gain_copy(peer_mp(k), peer_mp(k)).wait_recv(), 1)
+        all_gains().wait_recv()
 
     def other_weights():
         loop(half, lambda k: w_copy(2 * k + 1 - odd, partner, False).wait_recv())
@@ -862,7 +872,7 @@
         @pl.when(is_end)
         def _():
             up = jnp.where(me == 0, 1, 0)
-            loop(pieces, lambda c: tok_copy(me, c, up).wait_send())
+            tokens_sent(me, up)
             both_ways(release)
             by_shard()
 
@@ -943,39 +953,27 @@
             ctx_copy(me, i).start()
 
     def drain_line(s):
-        @pl.when(s != me)
-        def _():
-            gain_copy(me, s).wait_send()
-
-        def one(c):
-            waited = (odd == 0) & (s == me) & is_end
-
-            @pl.when((s <= me) & (me < n - 1) & jnp.logical_not(waited))
-            def _():
-                tok_copy(s, c, 1).wait_send()
-
-            @pl.when((s >= me) & (me > 0) & jnp.logical_not(waited))
-            def _():
-                tok_copy(s, c, 0).wait_send()
-
-        loop(pieces, one)
+        waited = (odd == 0) & (s == me) & is_end
+
+        @pl.when((s <= me) & (me < n - 1) & jnp.logical_not(waited))
+        def _():
+            tokens_sent(s, 1)
+
+        @pl.when((s >= me) & (me > 0) & jnp.logical_not(waited))
+        def _():
+            tokens_sent(s, 0)
 
         @pl.when(is_source)
         def _():
-            o_copy(s, d, partner, False).wait_send()
-            loop(half, lambda k: o_copy(s, d, same_core(k), False).wait_send(), 1)
+            sent(wo_all.at[s], o_send.at[0, s])
 
     def drain_early():
+        all_gains().wait_send()
         loop(n, drain_line)
-        w_copy(d, partner, False).wait_send()
-
-        def drain_weights(k):
-            w_copy(d, same_core(k), False).wait_send()
-            w_copy(from_core(k), partner, True).wait_send()
-
-        loop(half, drain_weights, 1)
+        sent(w_all.at[:, pl.ds(0, half * wrows), :], w_send.at[0])
+        sent(w_all.at[:, pl.ds(0, (half - 1) * wrows), :], w_send.at[1])
         pl.when(jnp.logical_not(is_source))(lambda: cross_copy().wait_send())
-        loop(chunks, lambda c: ctx_copy(me, c).wait_send())
+        sent(ctx_all.at[me], ctx_send.at[0])
 
     def project_out(s, at, first=False):
         weight = jnp.concatenate([wo_all[s, i] for i in range(wo_all.shape[1])], axis=1)
@@ -1059,22 +1057,17 @@
 
     loop(chunks, normalize)
 
-    def drain_late(c):
-        ctx_copy(near_end, c).wait_send()
-        end_copy(c).wait_send()
-        loop(n, lambda k: ss_copy(me, c, peer_mp(k)).wait_send(), 1)
-
     def drain_slices(z):
-        def forwarded(k):
-            o = from_core(k)
-            pl.when(in_plane(o))(lambda: o_copy(z, o, partner, True).wait_send())
-
-        loop(half, forwarded, 1)
+        spreads = is_source
+        pl.when(spreads)(lambda: sent(wo_all.at[z, pl.ds(0, half // 2 - 1)], o_send.at[1, z]))
+        pl.when(jnp.logical_not(spreads))(lambda: sent(wo_all.at[z, pl.ds(0, half // 2)], o_send.at[1, z]))
 
     @pl.when(is_inner)
     def _():
         drain_early()
-        loop(chunks, drain_late)
+        sent(ctx_all.at[near_end], ctx_send.at[1])
+        sent(out_buf, end_send.at[0])
+        sent(ss_all.at[pl.ds(0, n - 1)], ss_send.at[0])
         loop(n, drain_slices)
 
 
@@ -1120,21 +1113,21 @@
             pltpu.VMEM((rows, feats), BF16),
             pltpu.VMEM((chunks, 8, step), F32),
             pltpu.VMEM((n, chunks, 8, step), F32),
-            dma((2, n, pieces)),
+            dma((2, n)),
             dma((n, pieces)),
-            dma((n,)),
-            dma((n,)),
-            dma((2, groups)),
+            dma((1,)),
+            dma((1,)),
+            dma((2,)),
             dma((groups,)),
             dma((1,)),
-            dma((2, n, groups)),
-            dma((n, groups)),
+            dma((2, n)),
+            dma((n, groups // 2)),
+            dma((2,)),
             dma((n, chunks)),
-            dma((n, chunks)),
+            dma((1,)),
             dma((chunks,)),
-            dma((chunks,)),
-            dma((n, chunks)),
-            dma((n, chunks)),
+            dma((1,)),
+            dma((2, chunks)),
             dma((6,)),
             pltpu.SemaphoreType.REGULAR((2,)),
         ]

time: 41.9 us -> 40.2 us (0.959)
  Pallas kernels: 41.1 us -> 39.4 us
    pallas_call x1, Pallas kernels: 40.3 us -> 38.6 us  [on_device(): pl.pallas_call(body, out_shape=(pltpu.VMEM((rows, feats), BF16), pltpu.VM...]
where the time goes in v6:
time: 40.2 us; the launch traced here: 40 us
  Pallas kernels  39.4 us (98%)
  between operations  0.64 us (2%)
    pallas_call x1, Pallas kernels, on_device(): pl.pallas_call(body, out_shape=(pltpu.VMEM((rows, feats), BF16), pltpu.VM...  38.6 us
    pallas_call x1, Pallas kernels, on_device(): pl.pallas_call(publish, out_shape=(shape, shape), in_specs=[vmem] * 2, ou...  0.81 us

profile of v6, /device:TPU:1, one launch (start us, length us, event | category | flops | bytes accessed | tf_op | source)
XLA Modules:
  0.0 40.0 jit_solution(11427826759856262567)
XLA Ops:
  0.6 38.6 %shard_map.77 = (bf16[512,256]{1,0:T(8,128)(2,1)S(1)}, bf16[512,256]{1,0:T(8,128)(2,1)S(1)}) custom-call(bf16[512,256]{1,0:T(8,128)(2,1)} %tok.1, bf16[256]{0:T(256)(128)(2,1)} %pre.1, bf16[3,128,256]{2,1,0:T(8,128)(2,1)} %win.1, bf16[256,128]{1,0:T(8,128)(2,1)} %wout.1, bf16[4,512,512]{2,1,0:T(8,128)(2,1)} %bias.1, bf16[256]{0:T(256)(128)(2,1)} %post.1), custom_call_target="tpu_custom_call" | custom-call | tf_op jit(solution)/shard_map/pallas_call | solution.py:1170
  39.2 0.8 %shard_map.78 = (bf16[512,256]{1,0:T(8,128)(2,1)}, bf16[512,256]{1,0:T(8,128)(2,1)}) custom-call(bf16[512,256]{1,0:T(8,128)(2,1)S(1)} %get-tuple-element.4.stream_i, bf16[512,256]{1,0:T(8,128)(2,1)S(1)} %get-tuple-element.5.normed_i), custom_call_target="tpu_custom_call" | custom-call | tf_op jit(solution)/shard_map/pallas_call | solution.py:1181

commit v7 on v6

--- a/solution.py
+++ b/solution.py
@@ -629,7 +629,7 @@
         return remote(ref, ref, ag_send.at[up, s], ag_recv.at[s, c], {"mp": me + 2 * up - 1})
 
     def sent(ref, sem):
-        remote(ref, ref, sem, ctx_recv.at[0, 0], {"mp": inwards}).wait_send()
+        remote(ref, ref, sem, ctx_recv.at[0], {"mp": inwards}).wait_send()
 
     def tokens_sent(s, up):
         sent(x_all.at[s], ag_send.at[up, s])
@@ -653,15 +653,18 @@
         return wo_all.at[z, lax.rem(o, half)]
 
     def o_copy(z, o, target, forward):
-        send = o_send.at[1 if forward else 0, z]
+        send = o_send.at[1 if forward else 0]
         return remote(o_slot(z, o), o_slot(z, o), send, o_recv.at[z, lax.rem(o, half)], {"dp": target})
 
     def cross_copy():
         return remote(wo_own, o_slot(me, d), x_send.at[0], o_recv.at[me, lax.rem(d, half)], {"mp": home})
 
+    def ctx_place(s, c):
+        return jnp.where(s == 0, c, jnp.where(s == n - 1, chunks + c, 2 * chunks))
+
     def ctx_copy(s, c):
         ref = ctx_all.at[s, rows_at(c)]
-        return remote(ref, ref, ctx_send.at[jnp.where(s == me, 0, 1)], ctx_recv.at[s, c], {"mp": inwards})
+        return remote(ref, ref, ctx_send.at[jnp.where(s == me, 0, 1)], ctx_recv.at[ctx_place(s, c)], {"mp": inwards})
 
     def end_copy(c):
         return remote(
@@ -963,10 +966,6 @@
         def _():
             tokens_sent(s, 0)
 
-        @pl.when(is_source)
-        def _():
-            sent(wo_all.at[s], o_send.at[0, s])
-
     def drain_early():
         all_gains().wait_send()
         loop(n, drain_line)
@@ -1026,7 +1025,8 @@
         pl.when(odd == 0)(lambda: forward_slices(other_inner))
         loop(chunks, near, chunks // 2)
         other_slices(other_inner)
-        loop(chunks, lambda c: ctx_copy(other_inner, c).wait_recv())
+        ref = ctx_all.at[other_inner]
+        remote(ref, ref, ctx_send.at[0], ctx_recv.at[2 * chunks], {"mp": inwards}).wait_recv()
         project_out(other_inner, all_rows)
         other_slices(far_end)
 
@@ -1056,11 +1056,6 @@
         normed_o[rows_at(c), :] = (stream * scale * gain).astype(BF16)
 
     loop(chunks, normalize)
-
-    def drain_slices(z):
-        spreads = is_source
-        pl.when(spreads)(lambda: sent(wo_all.at[z, pl.ds(0, half // 2 - 1)], o_send.at[1, z]))
-        pl.when(jnp.logical_not(spreads))(lambda: sent(wo_all.at[z, pl.ds(0, half // 2)], o_send.at[1, z]))
 
     @pl.when(is_inner)
     def _():
@@ -1068,7 +1063,10 @@
         sent(ctx_all.at[near_end], ctx_send.at[1])
         sent(out_buf, end_send.at[0])
         sent(ss_all.at[pl.ds(0, n - 1)], ss_send.at[0])
-        loop(n, drain_slices)
+        few, many = pl.ds(0, half // 2 - 1), pl.ds(0, half // 2)
+        pl.when(is_source)(lambda: sent(wo_all, o_send.at[0]))
+        pl.when(is_source)(lambda: sent(wo_all.at[:, few], o_send.at[1]))
+        pl.when(jnp.logical_not(is_source))(lambda: sent(wo_all.at[:, many], o_send.at[1]))
 
 
 def publish(stream_i, normed_i, stream_o, normed_o, sems):
@@ -1120,10 +1118,10 @@
             dma((2,)),
             dma((groups,)),
             dma((1,)),
-            dma((2, n)),
+            dma((2,)),
             dma((n, groups // 2)),
             dma((2,)),
-            dma((n, chunks)),
+            dma((2 * chunks + 1,)),
             dma((1,)),
             dma((chunks,)),
             dma((1,)),

time: 40.2 us -> 40.1 us (level)
  no operation moved by 1% of the time
where the time goes in v7:
time: 40.1 us; the launch traced here: 39.9 us
  Pallas kernels  39.3 us (98%)
  between operations  0.64 us (2%)
    pallas_call x1, Pallas kernels, on_device(): pl.pallas_call(body, out_shape=(pltpu.VMEM((rows, feats), BF16), pltpu.VM...  38.5 us
    pallas_call x1, Pallas kernels, on_device(): pl.pallas_call(publish, out_shape=(shape, shape), in_specs=[vmem] * 2, ou...  0.81 us

profile of v7, /device:TPU:1, one launch (start us, length us, event | category | flops | bytes accessed | tf_op | source)
XLA Modules:
  0.0 39.9 jit_solution(16386495082841527671)
XLA Ops:
  0.6 38.5 %shard_map.77 = (bf16[512,256]{1,0:T(8,128)(2,1)S(1)}, bf16[512,256]{1,0:T(8,128)(2,1)S(1)}) custom-call(bf16[512,256]{1,0:T(8,128)(2,1)} %tok.1, bf16[256]{0:T(256)(128)(2,1)} %pre.1, bf16[3,128,256]{2,1,0:T(8,128)(2,1)} %win.1, bf16[256,128]{1,0:T(8,128)(2,1)} %wout.1, bf16[4,512,512]{2,1,0:T(8,128)(2,1)} %bias.1, bf16[256]{0:T(256)(128)(2,1)} %post.1), custom_call_target="tpu_custom_call" | custom-call | tf_op jit(solution)/shard_map/pallas_call | solution.py:1168
  39.1 0.8 %shard_map.78 = (bf16[512,256]{1,0:T(8,128)(2,1)}, bf16[512,256]{1,0:T(8,128)(2,1)}) custom-call(bf16[512,256]{1,0:T(8,128)(2,1)S(1)} %get-tuple-element.4.stream_i, bf16[512,256]{1,0:T(8,128)(2,1)S(1)} %get-tuple-element.5.normed_i), custom_call_target="tpu_custom_call" | custom-call | tf_op jit(solution)/shard_map/pallas_call | solution.py:1179

commit v8 on v7

--- a/solution.py
+++ b/solution.py
@@ -578,6 +578,7 @@
     step = rows // chunks
     pieces = ag_recv.shape[1]
     piece = rows // pieces
+    head = pieces // 8
     heads, seq = bias.shape[0], bias.shape[1]
     inner = win.shape[2]
     head_dim = inner // heads
@@ -726,8 +727,12 @@
             @pl.when(odd == 1)
             def _():
                 pl.semaphore_wait(link_free.at[up], 1)
-
-            loop(pieces, lambda c: tok_copy(me, c, up).start())
+                loop(pieces, lambda c: tok_copy(me, c, up).start(), head)
+
+            pl.when(odd == 0)(lambda: loop(pieces, lambda c: tok_copy(me, c, up).start()))
+
+    def send_head(up):
+        pl.when(can_send(up))(lambda: loop(head, lambda c: tok_copy(me, c, up).start()))
 
     def release(up):
         @pl.when(can_send(up))
@@ -912,6 +917,7 @@
             forward_slices(me)
 
     def gather_odd():
+        both_ways(send_head)
         send_weights()
         both_ways(send_own)
         by_shard()
@@ -948,8 +954,9 @@
             context = jnp.where(lane_head == h, mixed[h * step : (h + 1) * step], context)
         ctx_all[me, rows_at(c), :] = context.astype(BF16)
 
-    for c in range(0, chunks, 2):
-        together = range(c, min(c + 2, chunks))
+    starts = [0, *range(1, chunks, 2), chunks]
+    for c, stop in zip(starts[:-1], starts[1:]):
+        together = range(c, stop)
         for i in together:
             attend(i)
         for i in together:

time: 40.1 us -> 40 us (level)
  no operation moved by 1% of the time
where the time goes in v8:
time: 40 us; the launch traced here: 39.9 us
  Pallas kernels  39.2 us (98%)
  between operations  0.64 us (2%)
    pallas_call x1, Pallas kernels, on_device(): pl.pallas_call(body, out_shape=(pltpu.VMEM((rows, feats), BF16), pltpu.VM...  38.4 us
    pallas_call x1, Pallas kernels, on_device(): pl.pallas_call(publish, out_shape=(shape, shape), in_specs=[vmem] * 2, ou...  0.81 us

profile of v8, /device:TPU:1, one launch (start us, length us, event | category | flops | bytes accessed | tf_op | source)
XLA Modules:
  0.0 39.9 jit_solution(18061234259115059299)
XLA Ops:
  0.6 38.4 %shard_map.77 = (bf16[512,256]{1,0:T(8,128)(2,1)S(1)}, bf16[512,256]{1,0:T(8,128)(2,1)S(1)}) custom-call(bf16[512,256]{1,0:T(8,128)(2,1)} %tok.1, bf16[256]{0:T(256)(128)(2,1)} %pre.1, bf16[3,128,256]{2,1,0:T(8,128)(2,1)} %win.1, bf16[256,128]{1,0:T(8,128)(2,1)} %wout.1, bf16[4,512,512]{2,1,0:T(8,128)(2,1)} %bias.1, bf16[256]{0:T(256)(128)(2,1)} %post.1), custom_call_target="tpu_custom_call" | custom-call | tf_op jit(solution)/shard_map/pallas_call | solution.py:1175
  39.1 0.8 %shard_map.78 = (bf16[512,256]{1,0:T(8,128)(2,1)}, bf16[512,256]{1,0:T(8,128)(2,1)}) custom-call(bf16[512,256]{1,0:T(8,128)(2,1)S(1)} %get-tuple-element.4.stream_i, bf16[512,256]{1,0:T(8,128)(2,1)S(1)} %get-tuple-element.5.normed_i), custom_call_target="tpu_custom_call" | custom-call | tf_op jit(solution)/shard_map/pallas_call | solution.py:1186

commit v9 on v8

--- a/solution.py
+++ b/solution.py
@@ -992,7 +992,12 @@
 
     def finalize(c):
         def block(s, at):
-            stream = (x_all[s, rows_at(c), :].astype(F32) + part[rows_at(c), at]).astype(BF16)
+            slots = wo_all.shape[1] // 2
+            start = slots * (at.start // feats)
+            weight = jnp.concatenate([wo_all[far_end, start + i] for i in range(slots)], axis=1)
+            value = jnp.dot(ctx_all[far_end, rows_at(c), :], weight, preferred_element_type=F32)
+            value = x_all[s, rows_at(c), :].astype(F32) + (part[rows_at(c), at] + value)
+            stream = value.astype(BF16)
             wide_stream = stream.astype(F32)
             return stream, wide_stream * wide_stream
 
@@ -1039,7 +1044,6 @@
 
         def last(c):
             ctx_copy(far_end, c).wait_recv()
-            project_out(far_end, rows_at(c))
             finalize(c)
 
         loop(chunks, last)

time: 40 us -> 40 us (level)
  no operation moved by 1% of the time
where the time goes in v9:
time: 40 us; the launch traced here: 39.9 us
  Pallas kernels  39.2 us (98%)
  between operations  0.64 us (2%)
    pallas_call x1, Pallas kernels, on_device(): pl.pallas_call(body, out_shape=(pltpu.VMEM((rows, feats), BF16), pltpu.VM...  38.4 us
    pallas_call x1, Pallas kernels, on_device(): pl.pallas_call(publish, out_shape=(shape, shape), in_specs=[vmem] * 2, ou...  0.81 us

profile of v9, /device:TPU:1, one launch (start us, length us, event | category | flops | bytes accessed | tf_op | source)
XLA Modules:
  0.0 39.9 jit_solution(5323735163637977571)
XLA Ops:
  0.6 38.4 %shard_map.77 = (bf16[512,256]{1,0:T(8,128)(2,1)S(1)}, bf16[512,256]{1,0:T(8,128)(2,1)S(1)}) custom-call(bf16[512,256]{1,0:T(8,128)(2,1)} %tok.1, bf16[256]{0:T(256)(128)(2,1)} %pre.1, bf16[3,128,256]{2,1,0:T(8,128)(2,1)} %win.1, bf16[256,128]{1,0:T(8,128)(2,1)} %wout.1, bf16[4,512,512]{2,1,0:T(8,128)(2,1)} %bias.1, bf16[256]{0:T(256)(128)(2,1)} %post.1), custom_call_target="tpu_custom_call" | custom-call | tf_op jit(solution)/shard_map/pallas_call | solution.py:1179
  39.1 0.8 %shard_map.78 = (bf16[512,256]{1,0:T(8,128)(2,1)}, bf16[512,256]{1,0:T(8,128)(2,1)}) custom-call(bf16[512,256]{1,0:T(8,128)(2,1)S(1)} %get-tuple-element.4.stream_i, bf16[512,256]{1,0:T(8,128)(2,1)S(1)} %get-tuple-element.5.normed_i), custom_call_target="tpu_custom_call" | custom-call | tf_op jit(solution)/shard_map/pallas_call | solution.py:1190
